TPU v7x, 32 devices: a 4x2x2 block of a 4x4x8 slice. The times are simulated.
32 devices in a mesh: dp: 4 (over y, z), tp: 8 (over x, core).
Axes of the slice: x: 4, y: 2, z: 2, core: 2. Of those that a mesh axis runs over, the one named last changes fastest.
The devices are a block of a 4x4x8 slice.
Arguments:
- x_in: bfloat16 [8, 2048, 1024], P('dp', 'tp'), parts along dimension 0
- x_mid: bfloat16 [8, 2048, 1024], P('dp', 'tp'), parts along dimension 0
- d_out: bfloat16 [8, 2048, 1024], P('dp', 'tp'), parts along dimension 0
- q_saved: bfloat16 [8, 2048, 16, 64], P('dp', None, 'tp'), parts along dimension 0
- k_saved: bfloat16 [8, 2048, 16, 64], P('dp', None, 'tp'), parts along dimension 0
- v_saved: bfloat16 [8, 2048, 16, 64], P('dp', None, 'tp'), parts along dimension 0
- z_saved: bfloat16 [8, 2048, 4096], P('dp', None, 'tp'), parts along dimension 0
- ln1_gain: float32 [1024], replicated
- ln1_bias: float32 [1024], replicated
- ln2_gain: float32 [1024], replicated
- ln2_bias: float32 [1024], replicated
- w_qkv: bfloat16 [3, 1024, 16, 64], P(None, None, 'tp')
- w_proj: bfloat16 [16, 64, 1024], P('tp')
- w_fc1: bfloat16 [1024, 4096], P(None, 'tp')
- w_fc2: bfloat16 [4096, 1024], P('tp')
Outputs:
- output 1: bfloat16 [8, 2048, 1024], P('dp', 'tp'), parts along dimension 0
- output 2: float32 [12, 1024, 16, 64], P('dp', None, 'tp'), parts along dimension 0
- output 3: float32 [12, 16, 64], P('dp', 'tp'), parts along dimension 0
- output 4: float32 [64, 64, 1024], P(('dp', 'tp')), parts along dimension 0
- output 5: float32 [4096, 4096], P('dp', 'tp'), parts along dimension 0
- output 6: float32 [16384], P(('dp', 'tp')), parts along dimension 0
- output 7: float32 [16384, 1024], P(('dp', 'tp')), parts along dimension 0
- output 8: float32 [24, 1024], P('dp'), parts along dimension 0
There are 4 independent parts. A program takes and returns all parts, laid end to end along the dimension named above; an argument that names none is the same for every part.
All inputs are finite; a program needn't handle non-finite values.
Results may differ from a plain program's by a relative error of at most 0.0114087.
Values are sent between devices in bfloat16 or wider.
A program may use at most 768 MiB of HBM per device.

v0:
```python
import jax
import jax.numpy as jnp
from jax import lax
from jax.sharding import PartitionSpec as P

LN_EPS = 1e-5
GELU_COEF = 0.044715
GELU_SCALE = 0.7978845608028654


def layer_norm_fwd(token_rows, norm_gain, norm_bias):
    rows_f32 = token_rows.astype(jnp.float32)
    centered = rows_f32 - jnp.mean(rows_f32, axis=-1, keepdims=True)
    inv_std = lax.rsqrt(jnp.mean(centered * centered, axis=-1, keepdims=True) + LN_EPS)
    x_hat = centered * inv_std
    return x_hat, inv_std, (x_hat * norm_gain + norm_bias).astype(jnp.bfloat16)


def layer_norm_bwd(grad_norm, x_hat, inv_std, norm_gain):
    grad_hat = grad_norm * norm_gain
    centered_grad = grad_hat - jnp.mean(grad_hat, axis=-1, keepdims=True)
    return inv_std * (centered_grad - x_hat * jnp.mean(grad_hat * x_hat, axis=-1, keepdims=True))


def gelu_parts(pre_act):
    tanh_val = jnp.tanh(GELU_SCALE * (pre_act + GELU_COEF * pre_act * pre_act * pre_act))
    act_value = 0.5 * pre_act * (1.0 + tanh_val)
    act_slope = 0.5 * (1.0 + tanh_val) + 0.5 * pre_act * (1.0 - tanh_val * tanh_val) * GELU_SCALE * (1.0 + 3.0 * GELU_COEF * pre_act * pre_act)
    return act_value, act_slope


def attention_grads(q_heads, k_heads, v_heads, grad_ctx):
    seq_len = q_heads.shape[1]
    score_scale = q_heads.shape[-1] ** -0.5
    scores = jnp.einsum('bqhe,bkhe->bhqk', q_heads, k_heads, preferred_element_type=jnp.float32) * score_scale
    row_ids = lax.broadcasted_iota(jnp.int32, (seq_len, seq_len), 0)
    col_ids = lax.broadcasted_iota(jnp.int32, (seq_len, seq_len), 1)
    scores = jnp.where(row_ids >= col_ids, scores, -1e30)
    attn_probs = jax.nn.softmax(scores, axis=-1)
    probs_low = attn_probs.astype(jnp.bfloat16)
    context = jnp.einsum('bhqk,bkhe->bqhe', probs_low, v_heads, preferred_element_type=jnp.float32).astype(jnp.bfloat16)
    grad_probs = jnp.einsum('bqhe,bkhe->bhqk', grad_ctx, v_heads, preferred_element_type=jnp.float32)
    grad_scores = (attn_probs * (grad_probs - jnp.sum(grad_probs * attn_probs, axis=-1, keepdims=True)) * score_scale).astype(jnp.bfloat16)
    grad_q = jnp.einsum('bhqk,bkhe->bqhe', grad_scores, k_heads, preferred_element_type=jnp.float32).astype(jnp.bfloat16)
    grad_k = jnp.einsum('bhqk,bqhe->bkhe', grad_scores, q_heads, preferred_element_type=jnp.float32).astype(jnp.bfloat16)
    grad_v = jnp.einsum('bhqk,bqhe->bkhe', probs_low, grad_ctx, preferred_element_type=jnp.float32).astype(jnp.bfloat16)
    return context, grad_q, grad_k, grad_v


def solution(mesh):
    def local_backward(x_in, x_mid, d_out, q_saved, k_saved, v_saved, z_saved, ln1_gain, ln1_bias, ln2_gain, ln2_bias, w_qkv, w_proj, w_fc1, w_fc2):
        norm2_hat, norm2_rstd, h2_local = layer_norm_fwd(x_mid, ln2_gain, ln2_bias)
        h2_full = lax.all_gather(h2_local, 'tp', axis=1, tiled=True)
        dout_full = lax.all_gather(d_out, 'tp', axis=1, tiled=True)
        act_value, act_slope = gelu_parts(z_saved.astype(jnp.float32))
        grad_wfc2 = jnp.einsum('bsf,bsd->fd', act_value.astype(jnp.bfloat16), dout_full, preferred_element_type=jnp.float32)
        grad_pre = (jnp.einsum('bsd,fd->bsf', dout_full, w_fc2, preferred_element_type=jnp.float32) * act_slope).astype(jnp.bfloat16)
        grad_wfc1 = jnp.einsum('bsd,bsf->df', h2_full, grad_pre, preferred_element_type=jnp.float32)
        grad_bfc1 = jnp.sum(grad_pre, axis=(0, 1), dtype=jnp.float32)
        h2_partial = jnp.einsum('bsf,df->bsd', grad_pre, w_fc1, preferred_element_type=jnp.float32).astype(jnp.bfloat16)
        grad_h2 = lax.psum_scatter(h2_partial, 'tp', scatter_dimension=1, tiled=True).astype(jnp.float32)
        grad_mid = (d_out.astype(jnp.float32) + layer_norm_bwd(grad_h2, norm2_hat, norm2_rstd, ln2_gain)).astype(jnp.bfloat16)
        mid_full = lax.all_gather(grad_mid, 'tp', axis=1, tiled=True)
        norm1_hat, norm1_rstd, h1_local = layer_norm_fwd(x_in, ln1_gain, ln1_bias)
        h1_full = lax.all_gather(h1_local, 'tp', axis=1, tiled=True)
        grad_ctx = jnp.einsum('bsd,hed->bshe', mid_full, w_proj, preferred_element_type=jnp.float32).astype(jnp.bfloat16)
        context, grad_q, grad_k, grad_v = attention_grads(q_saved, k_saved, v_saved, grad_ctx)
        grad_wproj = jnp.einsum('bshe,bsd->hed', context, mid_full, preferred_element_type=jnp.float32)
        qkv_grads = jnp.stack([grad_q, grad_k, grad_v])
        grad_wqkv = jnp.einsum('bsd,ibshe->idhe', h1_full, qkv_grads, preferred_element_type=jnp.float32)
        grad_bqkv = jnp.sum(qkv_grads, axis=(1, 2), dtype=jnp.float32)
        h1_partial = jnp.einsum('ibshe,idhe->bsd', qkv_grads, w_qkv, preferred_element_type=jnp.float32).astype(jnp.bfloat16)
        grad_h1 = lax.psum_scatter(h1_partial, 'tp', scatter_dimension=1, tiled=True).astype(jnp.float32)
        grad_x = (grad_mid.astype(jnp.float32) + layer_norm_bwd(grad_h1, norm1_hat, norm1_rstd, ln1_gain)).astype(jnp.bfloat16)
        vec_partial = jnp.stack([
            jnp.sum(grad_h1 * norm1_hat, axis=(0, 1)),
            jnp.sum(grad_h1, axis=(0, 1)),
            jnp.sum(grad_h2 * norm2_hat, axis=(0, 1)),
            jnp.sum(grad_h2, axis=(0, 1)),
            jnp.sum(grad_mid, axis=(0, 1), dtype=jnp.float32),
            jnp.sum(d_out, axis=(0, 1), dtype=jnp.float32),
        ])
        grad_vecs = lax.psum(vec_partial, 'tp')
        return grad_x, grad_wqkv, grad_bqkv, grad_wproj, grad_wfc1, grad_bfc1, grad_wfc2, grad_vecs

    tok_spec = P('dp', 'tp', None)
    head_spec = P('dp', None, 'tp', None)
    in_specs = (tok_spec, tok_spec, tok_spec, head_spec, head_spec, head_spec, P('dp', None, 'tp'),
                P(None), P(None), P(None), P(None),
                P(None, None, 'tp', None), P('tp', None, None), P(None, 'tp'), P('tp', None))
    out_specs = (tok_spec, P('dp', None, 'tp', None), P('dp', 'tp', None), P(('dp', 'tp'), None, None),
                 P('dp', 'tp'), P(('dp', 'tp')), P(('dp', 'tp'), None), P('dp', None))
    return jax.shard_map(local_backward, mesh=mesh, in_specs=in_specs, out_specs=out_specs, check_vma=False)
```

profile of v0, /device:TPU:81, one launch (start us, length us, event | category | flops | bytes accessed | tf_op | source)
XLA Modules:
  0.0 598.7 jit_solution(14727005737971113828)
XLA Ops:
  7.2 0.0 copy-start
  7.2 0.1 all-gather.5.cloned.1.call-start
  7.3 0.7 all-gather.5.cloned.1.call-update
  8.0 0.0 copy-start.19
  8.0 0.1 reduce-scatter.3.cloned.1.call-start
  8.1 52.5 %all-gather.5.cloned.1.call-done = bf16[2,2048,1024]{2,1,0:T(8,128)(2,1)} async-done(((bf16[2,256,1024]{2,1,0:T(8,128)(2,1)}), bf16[2,2048,1024]{2,1,0:T(8,128)(2,1)}) %all-gather.5.cloned.1.call-update) | async-done | bytes 8388624 | tf_op jit(solution)/shard_map/all_gather | solution.py:54
  60.6 13.6 %convert_reduce_fusion = (f32[512]{0:T(512)}, bf16[2,2048,512]{2,1,0:T(8,128)(2,1)S(1)}) fusion(bf16[2,2048,512]{2,1,0:T(8,128)(2,1)} %param.21, bf16[2,2048,1024]{2,1,0:T(8,128)(2,1)} %all-gather.5.cloned.1.call-done, bf16[512,1024]{1,0:T(8,128)(2,1)} %param.29), kind=kOutput, calls=%fused_computation.42 | convolution fusion | flops 4341104128 | bytes 17827840 | tf_op jit(solution)/shard_map/bsd,fd->bsf/dot_general | solution.py:57
  74.2 2.0 copy-done.22
  76.3 0.0 copy-done.19
  76.3 7.2 %convolution_convert_fusion = bf16[2,2048,1024]{2,1,0:T(8,128)(2,1)} fusion(bf16[2,2048,512]{2,1,0:T(8,128)(2,1)S(1)} %get-tuple-element.24, bf16[1024,512]{1,0:T(8,128)(2,1)S(1)} %copy-done.19), kind=kOutput, calls=%fused_computation.45 | convolution fusion | flops 4299161600 | bytes 13631488 | tf_op jit(solution)/shard_map/bsf,df->bsd/dot_general | solution.py:60
  83.5 0.1 reduce-scatter.3.cloned.1.call-update
  83.5 0.1 all-gather.7.cloned.1.call-start
  83.6 1.1 copy-done.4
  84.7 0.2 convert_reduce_fusion.6
  84.9 0.4 fusion.85
  85.3 47.1 %reduce-scatter.3.cloned.1.call-done = bf16[2,256,1024]{2,1,0:T(8,128)(2,1)} async-done(((bf16[2,2048,1024]{2,1,0:T(8,128)(2,1)}), bf16[2,256,1024]{2,1,0:T(8,128)(2,1)}) %reduce-scatter.3.cloned.1.call-update) | async-done | bytes 1048592 | tf_op jit(solution)/shard_map/reduce_scatter | solution.py:61
  132.5 0.0 copy-done.11
  132.5 0.0 copy-done.17
  132.5 3.8 fusion.90
  136.3 0.0 copy-done.7
  136.3 3.9 convert_reduce_fusion.5
  140.2 0.1 all-gather.7.cloned.1.call-update
  140.3 0.5 reduce-scatter.5.cloned.1.call-start
  140.8 4.1 iota_compare_fusion
  144.9 33.5 %fusion.121 = (f32[2,2,2048]{2,1,0:T(2,128)S(1)}, f32[2,2,2048,2048]{2,3,1,0:T(8,128)}) fusion(pred[2048,2048]{0,1:T(8,128)(4,1)} %iota_compare_fusion, bf16[2,2048,2,64]{1,3,2,0:T(8,128)(2,1)} %param.18, bf16[2,2048,2,64]{1,3,2,0:T(8,128)(2,1)S(1)} %copy-done), kind=kOutput, calls=%fused_computation.129 | convolution fusion | flops 2214594560 | bytes 73433088 | tf_op jit(solution)/shard_map/sub | solution.py:39
  178.4 0.0 copy-start.21
  178.4 32.8 %fusion.119 = bf16[2,2,2048,2048]{2,3,1,0:T(8,128)(2,1)} fusion(f32[2,2,2048,2048]{2,3,1,0:T(8,128)} %get-tuple-element.22, f32[2,2,2048]{2,1,0:T(2,128)S(1)} %get-tuple-element.21), kind=kLoop, calls=%fused_computation.128 | loop fusion | flops 33554432 | bytes 100696064 | tf_op jit(solution)/shard_map/convert_element_type | solution.py:40
  211.2 0.0 all-gather.7.cloned.1.call-done
  211.2 0.0 copy-done.21
  211.2 6.3 %fusion.53 = bf16[2,2048,2,64]{1,3,2,0:T(8,128)(2,1)S(1)} fusion(bf16[2,2048,1024]{2,1,0:T(8,128)(2,1)} %all-gather.7.cloned.1.call-done, bf16[2,64,1024]{2,1,0:T(8,128)(2,1)S(1)} %copy-done.21), kind=kOutput, calls=%fused_computation.72 | convolution fusion | flops 1074266112 | bytes 9699328 | tf_op jit(solution)/shard_map/bsd,hed->bshe/dot_general | solution.py:66
  217.5 0.0 copy-start.2
  217.6 1.0 copy-done.2
  218.5 23.1 %fusion.122 = f32[2,2,2048,2048]{2,3,1,0:T(8,128)} fusion(bf16[2,2048,2,64]{1,3,2,0:T(8,128)(2,1)S(1)} %fusion.53, bf16[2,2048,2,64]{1,3,2,0:T(8,128)(2,1)S(1)} %copy-done.8), kind=kOutput, calls=%fused_computation.130 | convolution fusion | flops 2147483648 | bytes 69206016 | tf_op jit(solution)/shard_map/bqhe,bkhe->bhqk/dot_general | solution.py:42
  241.6 82.0 %fusion.73 = bf16[1,2,2048,2,64]{2,4,3,1,0:T(8,128)(2,1)S(1)} fusion(bf16[2,2048,2,64]{1,3,2,0:T(8,128)(2,1)S(1)} %copy-done, f32[2,2,2048,2048]{2,3,1,0:T(8,128)} %fusion.122, f32[2,2,2048,2048]{2,3,1,0:T(8,128)} %get-tuple-element.22, f32[2,2,2048]{2,1,0:T(2,128)S(1)} %get-tuple-element.21), kind=kOutput, calls=%fused_computation.84 | convolution fusion | flops 2265458688 | bytes 136347648 | tf_op jit(solution)/shard_map/bhqk,bkhe->bqhe/dot_general | solution.py:44
  323.6 0.0 copy-done.20
  323.6 0.0 copy-start.9
  323.6 0.0 copy-start.3
  323.6 82.5 %fusion.70 = bf16[1,2,2048,2,64]{2,4,3,1,0:T(8,128)(2,1)} fusion(bf16[2,2048,2,64]{1,3,2,0:T(8,128)(2,1)S(1)} %copy-done.20, f32[2,2,2048,2048]{2,3,1,0:T(8,128)} %fusion.122, f32[2,2,2048,2048]{2,3,1,0:T(8,128)} %get-tuple-element.22, f32[2,2,2048]{2,1,0:T(2,128)S(1)} %get-tuple-element.21), kind=kOutput, calls=%fused_computation.83 | convolution fusion | flops 2265458688 | bytes 136347648 | tf_op jit(solution)/shard_map/bhqk,bqhe->bkhe/dot_general | solution.py:45
  406.2 14.9 %fusion.64 = bf16[1,2,2048,2,64]{2,4,3,1,0:T(8,128)(2,1)S(1)} fusion(bf16[2,2048,2,64]{1,3,2,0:T(8,128)(2,1)S(1)} %copy-done.3, bf16[2,2,2048,2048]{2,3,1,0:T(8,128)(2,1)} %fusion.119), kind=kOutput, calls=%fused_computation.81 | convolution fusion | flops 2148007936 | bytes 35651584 | tf_op jit(solution)/shard_map/bhqk,bqhe->bkhe/dot_general | solution.py:46
  421.1 9.3 %bitcast_convert_fusion = bf16[2,2048,1024]{2,1,0:T(8,128)(2,1)} fusion(bf16[3,1024,2,64]{1,3,2,0:T(8,128)(2,1)} %param.26, bf16[1,2,2048,2,64]{2,4,3,1,0:T(8,128)(2,1)S(1)} %fusion.64, bf16[1,2,2048,2,64]{2,4,3,1,0:T(8,128)(2,1)} %fusion.70, bf16[1,2,2048,2,64]{2,4,3,1,0:T(8,128)(2,1)S(1)} %fusion.73), kind=kOutput, calls=%fused_computation.23 | convolution fusion | flops 3228565504 | bytes 12320768 | tf_op jit(solution)/shard_map/ibshe,idhe->bsd/dot_general | solution.py:72
  430.4 0.1 reduce-scatter.5.cloned.1.call-update
  430.5 0.1 all-gather.11.cloned.1.call-start
  430.5 0.6 all-gather.11.cloned.1.call-update
  431.1 0.3 all-gather.9.cloned.1.call-start
  431.4 0.2 copy-done.5
  431.6 0.2 convert_reduce_fusion.4
  431.8 0.4 fusion.80
  432.3 47.4 %reduce-scatter.5.cloned.1.call-done = bf16[2,256,1024]{2,1,0:T(8,128)(2,1)} async-done(((bf16[2,2048,1024]{2,1,0:T(8,128)(2,1)}), bf16[2,256,1024]{2,1,0:T(8,128)(2,1)}) %reduce-scatter.5.cloned.1.call-update) | async-done | bytes 1048592 | tf_op jit(solution)/shard_map/reduce_scatter | solution.py:73
  479.7 0.0 copy-done.12
  479.7 3.5 fusion.91
  483.2 0.1 all-gather.9.cloned.1.call-update
  483.2 0.0 copy-start.10
  483.2 10.7 %fusion.92 = f32[512,1024]{1,0:T(8,128)} fusion(bf16[2,2048,1024]{2,1,0:T(8,128)(2,1)} %all-gather.5.cloned.1.call-done, bf16[2,2048,512]{2,1,0:T(8,128)(2,1)} %param.21), kind=kOutput, calls=%fused_computation.101 | convolution fusion | flops 4315938816 | bytes 14680064 | tf_op jit(solution)/shard_map/bsf,bsd->fd/dot_general | solution.py:56
  494.0 0.0 copy-done.10
  494.0 1.1 convert_reduce_fusion.1
  495.1 33.6 %all-gather.11.cloned.1.call-done = bf16[2,2048,1024]{2,1,0:T(8,128)(2,1)} async-done(((bf16[2,256,1024]{2,1,0:T(8,128)(2,1)}), bf16[2,2048,1024]{2,1,0:T(8,128)(2,1)}) %all-gather.11.cloned.1.call-update) | async-done | bytes 8388624 | tf_op jit(solution)/shard_map/all_gather | solution.py:53
  528.7 10.4 %convolution_bitcast_fusion = f32[1024,512]{1,0:T(8,128)} fusion(bf16[2,2048,1024]{2,1,0:T(8,128)(2,1)} %all-gather.11.cloned.1.call-done, bf16[2,2048,512]{2,1,0:T(8,128)(2,1)} %copy-done.22), kind=kOutput, calls=%fused_computation.102 | convolution fusion | flops 4294967296 | bytes 14680064 | tf_op jit(solution)/shard_map/bsd,bsf->df/dot_general | solution.py:58
  539.1 0.0 copy-start.6
  539.1 17.0 %fusion.98 = f32[2,64,1024]{2,1,0:T(8,128)} fusion(bf16[2,2048,1024]{2,1,0:T(8,128)(2,1)} %all-gather.7.cloned.1.call-done, bf16[2,2,2048,2048]{2,3,1,0:T(8,128)(2,1)} %fusion.119, bf16[2,2048,2,64]{1,3,2,0:T(8,128)(2,1)} %param.20), kind=kOutput, calls=%fused_computation.104 | convolution fusion | flops 3221749760 | bytes 43515904 | tf_op jit(solution)/shard_map/bshe,bsd->hed/dot_general | solution.py:68
  556.1 0.0 copy-done.14
  556.1 0.1 stack.43
  556.2 23.5 %psum.7 = f32[6,1024]{1,0:T(8,128)} all-reduce(f32[6,1024]{1,0:T(8,128)S(1)} %stack.43), channel_id=1, replica_groups=mesh['dp'=4,'tp'=8] {'tp'}, use_global_device_ids=true, to_apply=%region_21.22 | all-reduce | flops 6144 | bytes 49152 | tf_op jit(solution)/shard_map/psum | solution.py:83
  579.7 3.1 fusion.87
  582.8 8.6 %fusion.95 = f32[3,1024,2,64]{1,3,2,0:T(8,128)} fusion(bf16[2,2048,1024]{2,1,0:T(8,128)(2,1)} %all-gather.9.cloned.1.call-done, bf16[1,2,2048,2,64]{2,4,3,1,0:T(8,128)(2,1)S(1)} %fusion.64, bf16[1,2,2048,2,64]{2,4,3,1,0:T(8,128)(2,1)} %fusion.70, bf16[1,2,2048,2,64]{2,4,3,1,0:T(8,128)(2,1)} %copy-done.9), kind=kOutput, calls=%fused_computation.103 | convolution fusion | flops 3224371200 | bytes 13107200 | tf_op jit(solution)/shard_map/bsd,ibshe->idhe/dot_general | solution.py:70
  (33 shorter events, 0.1 us)
Async XLA Ops:
  7.2 137.7 %copy-start = (bf16[2,2048,2,64]{1,3,2,0:T(8,128)(2,1)S(1)}, bf16[2,2048,2,64]{1,3,2,0:T(8,128)(2,1)}, u32[]{:S(2)}) copy-start(bf16[2,2048,2,64]{1,3,2,0:T(8,128)(2,1)} %param.19) | copy-start | bytes 3145732
  7.2 53.4 %all-gather.5.cloned.1.call-start = ((), (), s32[]{:S(2)}) async-start(), calls=%async_computation.2 | async-start | bytes 9437184 | tf_op jit(solution)/shard_map/all_gather | solution.py:54
  8.0 68.3 %copy-start.19 = (bf16[1024,512]{1,0:T(8,128)(2,1)S(1)}, bf16[1024,512]{1,0:T(8,128)(2,1)}, u32[]{:S(2)}) copy-start(bf16[1024,512]{1,0:T(8,128)(2,1)} %param.28) | copy-start | bytes 3145732
  8.0 124.5 %reduce-scatter.3.cloned.1.call-start = ((), (), s32[]{:S(2)}) async-start(), calls=%async_computation.3 | async-start | bytes 9437184 | tf_op jit(solution)/shard_map/reduce_scatter | solution.py:61
  74.2 2.0 copy-start.22
  83.5 1.2 copy-start.4
  83.5 49.0 %copy-start.11 = (f32[1024]{0:T(1024)S(1)}, f32[1024]{0:T(1024)}, u32[]{:S(2)}) copy-start(f32[1024]{0:T(1024)} %param.24) | copy-start | bytes 12292
  83.5 49.0 %copy-start.17 = (f32[1024]{0:T(1024)S(1)}, f32[1024]{0:T(1024)}, u32[]{:S(2)}) copy-start(f32[1024]{0:T(1024)} %param.25) | copy-start | bytes 12292
  83.5 52.9 %copy-start.7 = (bf16[2,256,1024]{2,1,0:T(8,128)(2,1)S(1)}, bf16[2,256,1024]{2,1,0:T(8,128)(2,1)}, u32[]{:S(2)}) copy-start(bf16[2,256,1024]{2,1,0:T(8,128)(2,1)} %param.17) | copy-start | bytes 3145732
  83.5 127.7 %all-gather.7.cloned.1.call-start = ((), (), s32[]{:S(2)}) async-start(), calls=%async_computation.4 | async-start | bytes 9437184 | tf_op jit(solution)/shard_map/all_gather | solution.py:63
  140.3 339.4 %reduce-scatter.5.cloned.1.call-start = ((), (), s32[]{:S(2)}) async-start(), calls=%async_computation.5 | async-start | bytes 9437184 | tf_op jit(solution)/shard_map/reduce_scatter | solution.py:73
  178.4 32.8 %copy-start.21 = (bf16[2,64,1024]{2,1,0:T(8,128)(2,1)S(1)}, bf16[2,64,1024]{2,1,0:T(8,128)(2,1)}, u32[]{:S(2)}) copy-start(bf16[2,64,1024]{2,1,0:T(8,128)(2,1)} %param.27) | copy-start | bytes 786436
  211.2 7.3 %copy-start.8 = (bf16[2,2048,2,64]{1,3,2,0:T(8,128)(2,1)S(1)}, bf16[2,2048,2,64]{1,3,2,0:T(8,128)(2,1)}, u32[]{:S(2)}) copy-start(bf16[2,2048,2,64]{1,3,2,0:T(8,128)(2,1)} %param.20) | copy-start | bytes 3145732
  217.5 1.0 copy-start.2
  241.6 82.0 %copy-start.20 = (bf16[2,2048,2,64]{1,3,2,0:T(8,128)(2,1)S(1)}, bf16[2,2048,2,64]{1,3,2,0:T(8,128)(2,1)}, u32[]{:S(2)}) copy-start(bf16[2,2048,2,64]{1,3,2,0:T(8,128)(2,1)} %param.18) | copy-start | bytes 3145732
  323.6 170.4 %copy-start.9 = (bf16[1,2,2048,2,64]{2,4,3,1,0:T(8,128)(2,1)}, bf16[1,2,2048,2,64]{2,4,3,1,0:T(8,128)(2,1)S(1)}, u32[]{:S(2)}) copy-start(bf16[1,2,2048,2,64]{2,4,3,1,0:T(8,128)(2,1)S(1)} %fusion.73) | copy-start | bytes 3145732
  323.6 82.5 %copy-start.3 = (bf16[2,2048,2,64]{1,3,2,0:T(8,128)(2,1)S(1)}, bf16[2,2048,2,64]{1,3,2,0:T(8,128)(2,1)}, u32[]{:S(2)}) copy-start(bf16[2,2048,2,64]{1,3,2,0:T(8,128)(2,1)} %copy-done.2) | copy-start | bytes 3145732
  430.4 1.2 copy-start.5
  430.4 49.3 %copy-start.12 = (f32[1024]{0:T(1024)S(1)}, f32[1024]{0:T(1024)}, u32[]{:S(2)}) copy-start(f32[1024]{0:T(1024)} %param.22) | copy-start | bytes 12292
  430.4 49.3 %copy-start.18 = (f32[1024]{0:T(1024)S(1)}, f32[1024]{0:T(1024)}, u32[]{:S(2)}) copy-start(f32[1024]{0:T(1024)} %param.23) | copy-start | bytes 12292
  430.5 98.2 %all-gather.11.cloned.1.call-start = ((), (), s32[]{:S(2)}) async-start(), calls=%async_computation.7 | async-start | bytes 9437184 | tf_op jit(solution)/shard_map/all_gather | solution.py:53
  431.1 151.7 %all-gather.9.cloned.1.call-start = ((), (), s32[]{:S(2)}) async-start(), calls=%async_computation.6 | async-start | bytes 9437184 | tf_op jit(solution)/shard_map/all_gather | solution.py:65
  483.2 10.7 %copy-start.10 = (bf16[1,2,2048,2,64]{2,4,3,1,0:T(8,128)(2,1)S(1)}, bf16[1,2,2048,2,64]{2,4,3,1,0:T(8,128)(2,1)}, u32[]{:S(2)}) copy-start(bf16[1,2,2048,2,64]{2,4,3,1,0:T(8,128)(2,1)} %fusion.70) | copy-start | bytes 3145732
  539.1 17.0 %copy-start.13 = (f32[1024]{0:T(1024)S(1)}, f32[1024]{0:T(1024)}, u32[]{:S(2)}) copy-start(f32[1024]{0:T(1024)} %get-tuple-element.8) | copy-start | bytes 12292
  539.1 17.0 %copy-start.14 = (f32[1024]{0:T(1024)S(1)}, f32[1024]{0:T(1024)}, u32[]{:S(2)}) copy-start(f32[1024]{0:T(1024)} %get-tuple-element.14) | copy-start | bytes 12292
  539.1 17.0 %copy-start.15 = (f32[1024]{0:T(1024)S(1)}, f32[1024]{0:T(1024)}, u32[]{:S(2)}) copy-start(f32[1024]{0:T(1024)} %get-tuple-element.16) | copy-start | bytes 12292
  539.1 17.0 %copy-start.16 = (f32[1024]{0:T(1024)S(1)}, f32[1024]{0:T(1024)}, u32[]{:S(2)}) copy-start(f32[1024]{0:T(1024)} %get-tuple-element.20) | copy-start | bytes 12292
  539.1 40.6 %copy-start.6 = (bf16[2,256,1024]{2,1,0:T(8,128)(2,1)S(1)}, bf16[2,256,1024]{2,1,0:T(8,128)(2,1)}, u32[]{:S(2)}) copy-start(bf16[2,256,1024]{2,1,0:T(8,128)(2,1)} %get-tuple-element.17) | copy-start | bytes 3145732
  582.8 8.7 %copy-start.1 = (bf16[2,2048,2,64]{1,3,2,0:T(8,128)(2,1)S(1)}, bf16[2,2048,2,64]{1,3,2,0:T(8,128)(2,1)}, u32[]{:S(2)}) copy-start(bf16[2,2048,2,64]{1,3,2,0:T(8,128)(2,1)} %param.19) | copy-start | bytes 3145732
Sparse Core Ops, SparseCore 0:
  9.6 50.9 all-gather.4
  83.7 48.7 reduce-scatter.2
  140.4 46.8 all-gather.6
  430.6 49.0 reduce-scatter.4
  481.7 46.8 all-gather.10
  530.1 46.8 all-gather.8
where the time goes:
time: 609 us; the launch traced here: 599 us
  matrix products  319 us (52%)
  waiting for transfers between devices  182 us (30%)
  other arithmetic  53.6 us (9%)
  blocking collectives  23.5 us (4%)
  between operations  14.7 us (2%)
    dot_general x1, matrix products, attention_grads(): jnp.einsum('bhqk,bqhe->bkhe', grad_scores, q_heads, preferred_element_typ...  82.5 us
    dot_general x1, matrix products, attention_grads(): jnp.einsum('bhqk,bkhe->bqhe', grad_scores, k_heads, preferred_element_typ...  82 us
    all_gather x1, waiting for transfers between devices, local_backward(): dout_full = lax.all_gather(d_out, 'tp', axis=1, tiled=True)  52.5 us
    reduce_scatter x1, waiting for transfers between devices, local_backward(): lax.psum_scatter(h1_partial, 'tp', scatter_dimension=1, tiled=True)  47.4 us
    reduce_scatter x1, waiting for transfers between devices, local_backward(): lax.psum_scatter(h2_partial, 'tp', scatter_dimension=1, tiled=True)  47.1 us
    all_gather x1, waiting for transfers between devices, local_backward(): h2_full = lax.all_gather(h2_local, 'tp', axis=1, tiled=True)  33.6 us
    sub x1, matrix products, attention_grads(): attn_probs = jax.nn.softmax(scores, axis=-1)  33.5 us
    convert_element_type x1, other arithmetic, attention_grads(): probs_low = attn_probs.astype(jnp.bfloat16)  32.8 us
  transfers between devices with their start and end apart: 6, of which 4 were waited for; matrix products, arithmetic and copies ran while one was open for 20% of the time, Pallas kernels for 0%

commit v1 on v0

v1 whole, which is shorter than its diff:
```python
import functools

import jax
import jax.numpy as jnp
from jax import lax
from jax.experimental import pallas as pl
from jax.experimental.pallas import tpu as pltpu
from jax.sharding import PartitionSpec as P

LN_EPS = 1e-5
GELU_COEF = 0.044715
GELU_SCALE = 0.7978845608028654
LOG2E = 1.4426950408889634
MESH = pl.DeviceIdType.MESH
F32 = jnp.float32
BF16 = jnp.bfloat16
VMEM_LIMIT = 67043328

NN = (((1,), (0,)), ((), ()))
NT = (((1,), (1,)), ((), ()))
TN = (((0,), (0,)), ((), ()))

CORES = 2
BATCH = range(2)
HEADS = range(2)
RING = R_RIGHT, R_FAR, R_LEFT = 1, 2, 3
SLOT_P, SLOT_R, SLOT_F, SLOT_L, SLOT_END = 1, 2, 4, 6, 8
PARTNER, RIGHT, LEFT, FWD_R, FWD_L = range(5)
NEAR_R, NEAR_L, FAR_R, FAR_L, LAST_R, LAST_L = range(4, 10)
SUB = 8
LANES = 128
TK = 512
NC = 256
STEP = 64


def mm(a, b, dims):
    return lax.dot_general(a, b, dims, preferred_element_type=F32)


def loop(count, body):
    def run(i, carry):
        body(i)
        return carry
    lax.fori_loop(0, count, run, 0)


def fold8(v):
    return jnp.sum(v.reshape(v.shape[0] // SUB, SUB, v.shape[1]), axis=0)


def turn(v):
    return jnp.transpose(v.astype(F32)).astype(BF16)


def span(i, size):
    return pl.ds(pl.multiple_of(i * size, size), size)


def columns(width):
    return [pl.ds(n * NC, NC) for n in range(width // NC)]


def clear(*refs):
    for ref in refs:
        ref[...] = jnp.zeros_like(ref)


def ln_stats(rows):
    centered = rows - jnp.mean(rows, axis=-1, keepdims=True)
    inv_std = lax.rsqrt(jnp.mean(centered * centered, axis=-1, keepdims=True) + LN_EPS)
    return centered * inv_std, inv_std


def ln_bwd(grad, x_hat, inv_std, gain):
    grad_hat = grad * gain
    centered = grad_hat - jnp.mean(grad_hat, axis=-1, keepdims=True)
    return inv_std * (centered - x_hat * jnp.mean(grad_hat * x_hat, axis=-1, keepdims=True))


def normalize(src, dst, gain, bias):
    per = src.shape[1] // STEP

    def body(i):
        b, rs = i // per, span(lax.rem(i, per), STEP)
        x_hat, _ = ln_stats(src[b, rs].astype(F32))
        dst[0, b, rs] = (x_hat * gain[...] + bias[...]).astype(BF16)

    loop(len(BATCH) * per, body)


def start_copies(pairs, sems):
    copies = [pltpu.make_async_copy(s, d, sems.at[i]) for i, (s, d) in enumerate(pairs)]
    for copy in copies:
        copy.start()
    return copies


class Place:
    def __init__(self, n_tp):
        self.chips = n_tp // CORES
        me = lax.axis_index('tp')
        self.x = me // CORES
        self.c = lax.rem(me, CORES)
        self.partner = self.block(0, 1)
        self.right, self.far, self.left = [self.block(r, 0) for r in RING]

    def block(self, r, p):
        return lax.rem(self.x + r, self.chips) * CORES + lax.rem(self.c + p, CORES)

    def enter(self, peers):
        barrier = pltpu.get_barrier_semaphore()
        for peer in peers:
            pl.semaphore_signal(barrier, inc=1, device_id={'tp': peer}, device_id_type=MESH)
        pl.semaphore_wait(barrier, len(peers))


def remote(src, dst, ssem, rsem, peer):
    return pltpu.make_async_remote_copy(src_ref=src, dst_ref=dst, send_sem=ssem, recv_sem=rsem,
                                        device_id={'tp': peer}, device_id_type=MESH)


class Gather:
    def __init__(self, place, own, buf, ssem, rsem):
        self.place, self.own, self.buf, self.ssem, self.rsem = place, own, buf, ssem, rsem
        half = buf.shape[-2] // 2
        self.lo, self.hi = pl.ds(0, half), pl.ds(half, half)

    def _own(self, kind, slot, b, peer):
        return remote(self.own.at[b], self.buf.at[slot, b], self.ssem.at[kind, b], self.rsem.at[slot, b], peer)

    def to_partner(self, b):
        return self._own(PARTNER, SLOT_P, b, self.place.partner)

    def to_right(self, b):
        return self._own(RIGHT, SLOT_L, b, self.place.right)

    def to_left(self, b):
        return self._own(LEFT, SLOT_R, b, self.place.left)

    def fwd_right(self, b):
        return remote(self.buf.at[SLOT_L, b, self.lo], self.buf.at[SLOT_F, b, self.lo],
                      self.ssem.at[FWD_R, b], self.rsem.at[SLOT_F, b], self.place.right)

    def fwd_left(self, b):
        return remote(self.buf.at[SLOT_R, b, self.hi], self.buf.at[SLOT_F, b, self.hi],
                      self.ssem.at[FWD_L, b], self.rsem.at[SLOT_END, b], self.place.left)

    def share(self, r, b):
        slot = CORES * r
        return remote(self.buf.at[slot, b], self.buf.at[slot + 1, b], self.ssem.at[FWD_L + r, b], self.rsem.at[slot + 1, b],
                      self.place.partner)

    def start_own(self, b):
        self.to_right(b).start()
        self.to_left(b).start()
        self.to_partner(b).start()

    def relay(self, b):
        self.to_right(b).wait_recv()
        self.fwd_right(b).start()
        self.to_left(b).wait_recv()
        self.fwd_left(b).start()
        self.share(R_LEFT, b).start()
        self.share(R_RIGHT, b).start()

    def relay_far(self, b):
        self.fwd_right(b).wait_recv()
        self.fwd_left(b).wait_recv()
        self.share(R_FAR, b).start()

    def wait_shared(self, r, b):
        self.share(r, b).wait_recv()

    def wait_partner(self, b):
        self.to_partner(b).wait_recv()

    def finish(self):
        for b in BATCH:
            for copy in (self.to_partner(b), self.to_right(b), self.to_left(b), self.fwd_right(b), self.fwd_left(b),
                         *(self.share(r, b) for r in RING)):
                copy.wait_send()


class Scatter:
    def __init__(self, place, p_out, p_in, sums, fin, transit, ssem, rsem):
        self.place = place
        self.p_out, self.p_in, self.sums, self.fin, self.transit = p_out, p_in, sums, fin, transit
        self.ssem, self.rsem = ssem, rsem
        half = sums.shape[-2] // 2
        self.lo, self.hi = pl.ds(0, half), pl.ds(half, half)

    def to_partner(self, r, b):
        return remote(self.p_out.at[r, b], self.p_in.at[r, b], self.ssem.at[r, b], self.rsem.at[r, b], self.place.partner)

    def _hop(self, kind, src, dst, b, peer):
        return remote(src, dst, self.ssem.at[kind, b], self.rsem.at[kind, b], peer)

    def near_right(self, b):
        return self._hop(NEAR_R, self.sums.at[0, b, self.hi], self.fin.at[0, b, self.hi], b, self.place.right)

    def near_left(self, b):
        return self._hop(NEAR_L, self.sums.at[2, b, self.lo], self.fin.at[1, b, self.lo], b, self.place.left)

    def far_right(self, b):
        return self._hop(FAR_R, self.sums.at[1, b, self.lo], self.transit.at[0, b], b, self.place.right)

    def far_left(self, b):
        return self._hop(FAR_L, self.sums.at[1, b, self.hi], self.transit.at[1, b], b, self.place.left)

    def last_right(self, b):
        return self._hop(LAST_R, self.sums.at[0, b, self.lo], self.fin.at[0, b, self.lo], b, self.place.right)

    def last_left(self, b):
        return self._hop(LAST_L, self.sums.at[2, b, self.hi], self.fin.at[1, b, self.hi], b, self.place.left)

    def send_near(self, b):
        self.near_right(b).start()
        self.near_left(b).start()

    def send_far(self, b):
        self.far_right(b).start()
        self.far_left(b).start()

    def send_last(self, b):
        for arrived, slot, lane, rows, onward in ((self.far_right, 0, 0, self.lo, self.last_right),
                                                  (self.far_left, 2, 1, self.hi, self.last_left)):
            arrived(b).wait_recv()
            self.sums[slot, b, rows] = (self.sums[slot, b, rows].astype(F32) + self.transit[lane, b].astype(F32)).astype(BF16)
            onward(b).start()

    def wait_final(self, b):
        for copy in (self.near_right, self.near_left, self.last_right, self.last_left):
            copy(b).wait_recv()

    def total(self, own, b, rs):
        return own[b, rs] + self.fin[0, b, rs].astype(F32) + self.fin[1, b, rs].astype(F32)

    def finish(self):
        for b in BATCH:
            for r in (0, *RING):
                self.to_partner(r, b).wait_send()
            for copy in (self.near_right, self.near_left, self.far_right, self.far_left, self.last_right, self.last_left):
                copy(b).wait_send()


def scatter_scratch(rows, width):
    def buf(*lead):
        return pltpu.VMEM((*lead, len(BATCH), rows, width), BF16)
    return [buf(4), buf(4), buf(3), buf(2), pltpu.VMEM((2, len(BATCH), rows // 2, width), BF16),
            pltpu.SemaphoreType.DMA((10, 2)), pltpu.SemaphoreType.DMA((10, 2))]


def gather_scratch(rows, width):
    return [pltpu.VMEM((SLOT_END, len(BATCH), rows, width), BF16),
            pltpu.SemaphoreType.DMA((SLOT_END, 2)), pltpu.SemaphoreType.DMA((SLOT_END + 1, 2))]


def first_head(shape):
    return lax.broadcasted_iota(jnp.int32, shape, 1) < shape[1] // len(HEADS)


def split_heads(v):
    first, zero = first_head(v.shape), jnp.zeros_like(v)
    return [jnp.where(first, v, zero), jnp.where(first, zero, v)]


def visible(blk, j, rows):
    row_id = blk * rows + lax.broadcasted_iota(jnp.int32, (rows, TK), 0)
    return row_id >= j * TK + lax.broadcasted_iota(jnp.int32, (rows, TK), 1)


def attn_fwd_block(b, blk, q_t, k_t, v_t, ctx_t, ctx, lse, s_buf, m_buf, scale):
    rows = ctx.shape[2]
    qs = span(blk, rows)
    last = blk // (TK // rows)
    q_h = split_heads(turn(q_t[b, :, qs]))

    def fold(f, v):
        parts = [v[:, i:i + LANES] for i in range(0, TK, LANES)]
        return functools.reduce(f, parts)

    def score(j, masked=False):
        kk = k_t[b, :, span(j, TK)]
        for h in HEADS:
            s = mm(q_h[h], kk, NN) * scale
            if masked:
                s = jnp.where(visible(blk, j, rows), s, -1e30)
            s_buf[h, :, span(j, TK)] = s
            top = fold(jnp.maximum, s)
            m_buf[h] = top if masked else jnp.maximum(m_buf[h], top)

    score(last, True)
    loop(last, score)
    m_col = [jnp.max(m_buf[h], axis=-1, keepdims=True) for h in HEADS]
    clear(m_buf)

    def total(j):
        for h in HEADS:
            m_buf[h] += fold(jnp.add, jnp.exp2(s_buf[h, :, span(j, TK)] - m_col[h]))

    loop(last + 1, total)
    l_col = [m_col[h] + jnp.log2(jnp.sum(m_buf[h], axis=-1, keepdims=True)) for h in HEADS]
    clear(m_buf)

    def weigh(j):
        vv = v_t[b, :, span(j, TK)]
        for h in HEADS:
            m_buf[h] += mm(jnp.exp2(s_buf[h, :, span(j, TK)] - l_col[h]).astype(BF16), vv, NT)

    loop(last + 1, weigh)
    first = first_head(m_buf.shape[1:])
    out = jnp.where(first, m_buf[0], m_buf[1])
    ctx[b, blk] = out
    lse[b, blk] = jnp.where(first, *l_col)
    ctx_t[b, :, qs] = turn(out)


def mlp_kernel(n_tp, scale, dy_hbm, xm_hbm, z_hbm, w1_hbm, w2_hbm, q_hbm, k_hbm, v_hbm, gain_ref, bias_ref,
               dx1_hbm, dw1_hbm, dw2_hbm, ctxt_hbm, ctx_hbm, lse_hbm, db1_ref, vec_ref,
               dyb, dy_ss, dy_rs, hb, h_ss, h_rs, p_out, p_in, sums, fin, transit, rs_ss, rs_rs,
               z, w1, w2, dw1, dw2, own, xm, db1, q_t, k_t, v_t, ctx_t, ctx, lse, s_buf, m_buf, lsem):
    place = Place(n_tp)
    rows, width = dy_hbm.shape[1:]
    units = w2.shape[0]
    blocks = ctx.shape[1]
    place.enter((place.partner, place.right, place.left))
    dyg = Gather(place, dy_hbm, dyb, dy_ss, dy_rs)
    hg = Gather(place, hb.at[0], hb, h_ss, h_rs)
    sc = Scatter(place, p_out, p_in, sums, fin, transit, rs_ss, rs_rs)
    for b in BATCH:
        dyg.start_own(b)
    loads = start_copies(((xm_hbm, xm), (dy_hbm, dyb.at[0]), (w2_hbm, w2), (z_hbm, z), (w1_hbm, w1),
                          (q_hbm, q_t), (k_hbm, k_t), (v_hbm, v_t)), lsem)
    clear(dw1, dw2, db1, vec_ref)
    loads[0].wait()
    normalize(xm, hb, gain_ref, bias_ref)
    for load in loads[1:]:
        load.wait()

    def attend(lo, count):
        def body(i):
            i = lo + i
            attn_fwd_block(i // blocks, lax.rem(i, blocks), q_t, k_t, v_t, ctx_t, ctx, lse, s_buf, m_buf, scale)
        loop(count, body)

    def pre_piece(r, p, b):
        dy, blk = dyb[CORES * r + p, b], place.block(r, p)
        for fs in columns(units):
            act = mm(dy, w2[fs, :], NT)
            zf = z[b, blk, :, fs].astype(F32)
            t = jnp.tanh(GELU_SCALE * (zf + GELU_COEF * zf * zf * zf))
            half_t = 0.5 * (1.0 + t)
            slope = half_t + 0.5 * zf * (1.0 - t * t) * GELU_SCALE * (1.0 + 3.0 * GELU_COEF * zf * zf)
            u = (zf * half_t).astype(BF16)
            dzv = (act * slope).astype(BF16)
            z[b, blk, :, fs] = dzv
            db1[:, fs] += fold8(dzv.astype(F32))
            dw2[fs, :] += mm(u, dy, TN)
        return z[b, blk]

    def pair(r, b, put):
        dz = pre_piece(r, 1, b)
        for ns in columns(width):
            p_out[r, b, :, ns] = mm(dz, w1[ns, :], NT).astype(BF16)
        sc.to_partner(r, b).start()
        dz = pre_piece(r, 0, b)
        sc.to_partner(r, b).wait_recv()
        for ns in columns(width):
            put(ns, mm(dz, w1[ns, :], NT) + p_in[r, b, :, ns].astype(F32))

    def pair_out(r, b):
        dyg.wait_shared(r, b)

        def put(ns, v):
            sums[r - 1, b, :, ns] = v.astype(BF16)
        pair(r, b, put)

    def own_body(b):
        dyg.wait_partner(b)

        def put(ns, v):
            own[b, :, ns] = v
        pair(0, b, put)

    def near_body(b):
        dyg.relay(b)
        loop(2, lambda i: pair_out(R_RIGHT + 2 * i, b))
        sc.send_near(b)
        attend(2 * b, 2)

    def far_body(b):
        dyg.relay_far(b)
        pair_out(R_FAR, b)
        sc.send_far(b)
        hg.start_own(b)

    def dw1_pair(r, b):
        def body(p):
            dw1[...] += mm(hb[CORES * r + p, b], z[b, place.block(r, p)], TN)
        loop(CORES, body)

    def dw1_own(b):
        hg.wait_partner(b)
        dw1_pair(0, b)

    def dw1_near(b):
        def body(i):
            r = R_RIGHT + 2 * i
            hg.wait_shared(r, b)
            dw1_pair(r, b)
        loop(2, body)

    def dw1_far(b):
        hg.relay_far(b)
        hg.wait_shared(R_FAR, b)
        dw1_pair(R_FAR, b)

    def back(b):
        sc.wait_final(b)

        def body(i):
            rs = span(i, STEP)
            grad = sc.total(own, b, rs)
            x_hat, inv_std = ln_stats(xm[b, rs].astype(F32))
            dyf = dyb[0, b, rs].astype(F32)
            dx1 = (dyf + ln_bwd(grad, x_hat, inv_std, gain_ref[...])).astype(BF16)
            xm[b, rs] = dx1
            for k, v in enumerate((grad * x_hat, grad, dx1.astype(F32), dyf)):
                vec_ref[k] += fold8(v)
        loop(rows // STEP, body)

    loop(2, own_body)
    loop(2, near_body)
    loop(2, far_body)
    rest = 2 * blocks - 4
    attend(4, rest)
    ctx_stores = start_copies(((ctx_t, ctxt_hbm), (ctx, ctx_hbm), (lse, lse_hbm)), lsem)
    loop(2, sc.send_last)
    hg.relay(0)
    loop(2, dw1_own)
    hg.relay(1)
    loop(2, dw1_near)
    loop(2, back)
    for store in ctx_stores:
        store.wait()
    stores = start_copies(((xm, dx1_hbm), (dw2, dw2_hbm)), lsem)
    db1_ref[...] = jnp.sum(db1[...], axis=0, keepdims=True)
    loop(2, dw1_far)
    for store in stores:
        store.wait()
    stores = start_copies(((dw1, dw1_hbm),), lsem)
    dyg.finish()
    hg.finish()
    sc.finish()
    stores[0].wait()


def mlp_backward(n_tp, scale, d_out, x_mid, z, w1, w2, q_t, k_t, v_t, gain, bias):
    batch, rows, width = d_out.shape
    units = w2.shape[0]
    seq = q_t.shape[2]
    blocks = seq // rows
    any_spec = pl.BlockSpec(memory_space=pl.ANY)
    vm = pl.BlockSpec(memory_space=pltpu.VMEM)
    heads_t = (batch, LANES, seq)
    per_row = (batch, blocks, rows, LANES)
    return pl.pallas_call(
        functools.partial(mlp_kernel, n_tp, scale),
        name='mlp_backward',
        out_shape=(jax.ShapeDtypeStruct((batch, rows, width), BF16), jax.ShapeDtypeStruct((width, units), F32),
                   jax.ShapeDtypeStruct((units, width), F32), jax.ShapeDtypeStruct(heads_t, BF16),
                   jax.ShapeDtypeStruct(per_row, F32), jax.ShapeDtypeStruct(per_row, F32),
                   jax.ShapeDtypeStruct((1, units), F32), jax.ShapeDtypeStruct((4, SUB, width), F32)),
        in_specs=[any_spec] * 8 + [vm] * 2,
        out_specs=(*[any_spec] * 6, vm, vm),
        scratch_shapes=gather_scratch(rows, width) + gather_scratch(rows, width) + scatter_scratch(rows, width) + [
            pltpu.VMEM((batch, blocks, rows, units), BF16),
            pltpu.VMEM((width, units), BF16), pltpu.VMEM((units, width), BF16),
            pltpu.VMEM((width, units), F32), pltpu.VMEM((units, width), F32),
            pltpu.VMEM((batch, rows, width), F32), pltpu.VMEM((batch, rows, width), BF16),
            pltpu.VMEM((SUB, units), F32), *[pltpu.VMEM(heads_t, BF16)] * 4, *[pltpu.VMEM(per_row, F32)] * 2,
            pltpu.VMEM((len(HEADS), rows, seq), F32), pltpu.VMEM((len(HEADS), rows, LANES), F32),
            pltpu.SemaphoreType.DMA((8,)),
        ],
        compiler_params=pltpu.CompilerParams(collective_id=1, has_side_effects=True, vmem_limit_bytes=VMEM_LIMIT),
    )(d_out, x_mid, z.reshape(batch, blocks, rows, units), w1, w2, q_t, k_t, v_t, gain.reshape(1, width), bias.reshape(1, width))


def attn_kernel(n_tp, scale, dx1_hbm, xi_hbm, q_hbm, k_hbm, v_hbm, ctxt_hbm, ctx_hbm, lse_hbm, wqkv_hbm, wo_hbm,
                gain_ref, bias_ref, vec_in,
                dx_hbm, dwqkv_hbm, dwo_hbm, dbqkv_ref, vecs_ref,
                mb, m_ss, m_rs, hb, h_ss, h_rs, p_out, p_in, sums, fin, transit, rs_ss, rs_rs,
                q_t, k_t, v_t, ctx_t, ctx, lse, wqkv, wo, dqkv, dk_acc, dv_acc, dq_acc,
                own, xi, dwqkv, dwo, vacc, vsend, vrecv, vring, lsem, v_ss, v_rs):
    place = Place(n_tp)
    rows, width = dx1_hbm.shape[1:]
    place.enter((place.partner, place.right, place.left, place.far))
    mg = Gather(place, dx1_hbm, mb, m_ss, m_rs)
    hg = Gather(place, hb.at[0], hb, h_ss, h_rs)
    sc = Scatter(place, p_out, p_in, sums, fin, transit, rs_ss, rs_rs)
    for b in BATCH:
        mg.start_own(b)
    loads = start_copies(((dx1_hbm, mb.at[0]), (wo_hbm, wo), (q_hbm, q_t), (k_hbm, k_t), (v_hbm, v_t), (ctx_hbm, ctx),
                          (lse_hbm, lse), (ctxt_hbm, ctx_t), (wqkv_hbm, wqkv), (xi_hbm, xi)), lsem)
    clear(dwqkv, dwo, dk_acc, dv_acc, vacc, vsend)
    for load in loads:
        load.wait()
    exp_scale = scale * LOG2E
    dim = LANES // len(HEADS)

    def attend(r, p, b):
        mid, blk = mb[CORES * r + p, b], place.block(r, p)
        qs = span(blk, rows)
        dwo[...] += mm(ctx_t[b, :, qs], mid, NN)
        dctx = mm(mid, wo[...], NT).astype(BF16)
        dctx_t = turn(dctx)
        qt = q_t[b, :, qs]
        q_h, d_h = split_heads(turn(qt)), split_heads(dctx)
        delta = [jnp.sum(v, axis=-1, keepdims=True) for v in split_heads(dctx.astype(F32) * ctx[b, blk])]
        lse_v = lse[b, blk]
        l_col = [lse_v[:, h * dim:h * dim + 1] for h in HEADS]
        last = blk // (TK // rows)
        clear(dq_acc)

        def tile(j, masked=False):
            ks = span(j, TK)
            kk, vv = k_t[b, :, ks], v_t[b, :, ks]
            for h in HEADS:
                hs = pl.ds(h * dim, dim)
                top = slice(h * dim, (h + 1) * dim)
                prob = jnp.exp2(mm(q_h[h], kk, NN) * exp_scale - l_col[h])
                if masked:
                    prob = jnp.where(visible(blk, j, rows), prob, 0.0)
                ds = (prob * (mm(d_h[h], vv, NN) - delta[h])).astype(BF16)
                dq_acc[h] += mm(ds, kk, NT)
                dk_acc[b, hs, ks] += mm(qt[top], ds, NN)
                dv_acc[b, hs, ks] += mm(dctx_t[top], prob.astype(BF16), NN)

        tile(last, True)
        loop(last, tile)
        dq = jnp.where(first_head(dq_acc.shape[1:]), dq_acc[0], dq_acc[1]) * scale
        dqkv[b, :LANES, qs] = turn(dq)

    def attend_own(b):
        mg.wait_partner(b)
        loop(CORES, lambda p: attend(0, p, b))

    def attend_near(b):
        mg.relay(b)
        for r in (R_RIGHT, R_LEFT):
            mg.wait_shared(r, b)
        loop(2 * CORES, lambda i: attend(R_RIGHT + 2 * (i // CORES), lax.rem(i, CORES), b))

    def partial_rows(r, p, b):
        return turn(dqkv[b, :, span(place.block(r, p), rows)])

    def reduce_out(r, b):
        lhs = partial_rows(r, 0, b)
        sc.to_partner(r, b).wait_recv()
        for ns in columns(width):
            sums[r - 1, b, :, ns] = (mm(lhs, wqkv[:, ns], NN) + p_in[r, b, :, ns].astype(F32)).astype(BF16)

    def attend_far(b):
        mg.relay_far(b)
        mg.wait_shared(R_FAR, b)
        loop(CORES, lambda p: attend(R_FAR, p, b))
        dqkv[b, LANES:2 * LANES] = (dk_acc[b] * scale).astype(BF16)
        dqkv[b, 2 * LANES:] = dv_acc[b].astype(BF16)

        def to_partner(i):
            r = lax.rem(R_FAR + i, place.chips)
            lhs = partial_rows(r, 1, b)
            for ns in columns(width):
                p_out[r, b, :, ns] = mm(lhs, wqkv[:, ns], NN).astype(BF16)
            sc.to_partner(r, b).start()

        loop(place.chips, to_partner)
        reduce_out(R_FAR, b)
        sc.send_far(b)
        loop(2, lambda i: reduce_out(R_RIGHT + 2 * i, b))
        sc.send_near(b)
        lhs = partial_rows(0, 0, b)
        sc.to_partner(0, b).wait_recv()
        for ns in columns(width):
            own[b, :, ns] = mm(lhs, wqkv[:, ns], NN) + p_in[0, b, :, ns].astype(F32)

    def dw_pair(r, b):
        def body(p):
            dwqkv[...] += mm(dqkv[b, :, span(place.block(r, p), rows)], hb[CORES * r + p, b], NN)
        loop(CORES, body)

    def dw_own(b):
        hg.wait_partner(b)
        dw_pair(0, b)

    def dw_near(b):
        def body(i):
            r = R_RIGHT + 2 * i
            hg.wait_shared(r, b)
            dw_pair(r, b)
        loop(2, body)

    def dw_far(b):
        hg.relay_far(b)
        hg.wait_shared(R_FAR, b)
        dw_pair(R_FAR, b)

    def back(b):
        sc.wait_final(b)

        def body(i):
            rs = span(i, STEP)
            grad = sc.total(own, b, rs)
            x_hat, inv_std = ln_stats(xi[b, rs].astype(F32))
            dx = (mb[0, b, rs].astype(F32) + ln_bwd(grad, x_hat, inv_std, gain_ref[...])).astype(BF16)
            xi[b, rs] = dx
            for k, v in enumerate((grad * x_hat, grad)):
                vacc[k] += fold8(v)
        loop(rows // STEP, body)

    loop(2, attend_own)
    normalize(xi, hb, gain_ref, bias_ref)
    loop(2, attend_near)
    hg.start_own(0)
    loop(2, attend_far)
    hg.start_own(1)
    loop(2, sc.send_last)
    hg.relay(0)
    loop(2, dw_own)
    ones = jnp.ones((SUB, dqkv.shape[2]), BF16)
    dbqkv_ref[...] = (mm(ones, dqkv[0], NT) + mm(ones, dqkv[1], NT))[:1]
    hg.relay(1)
    loop(2, dw_near)
    loop(2, back)
    stores = start_copies(((xi, dx_hbm), (dwo, dwo_hbm)), lsem)
    rows_in = [vacc[k] for k in range(vacc.shape[0])] + [vec_in[k] for k in range(vec_in.shape[0])]
    for k, v in enumerate(rows_in):
        vsend[k:k + 1] = jnp.sum(v, axis=0, keepdims=True)
    swap = remote(vsend, vrecv, v_ss.at[0], v_rs.at[n_tp], place.partner)
    swap.start()
    swap.wait_recv()
    vring[place.x] = vsend[...] + vrecv[...]
    ring = [remote(vring.at[place.x], vring.at[place.x], v_ss.at[r], v_rs.at[place.x], peer)
            for r, peer in zip(RING, (place.right, place.far, place.left))]
    for copy in ring:
        copy.start()
    loop(2, dw_far)
    stores += start_copies(((dwqkv, dwqkv_hbm),), lsem.at[pl.ds(2, 1)])
    for r in RING:
        other = lax.rem(place.x + r, place.chips)
        remote(vring.at[other], vring.at[other], v_ss.at[r], v_rs.at[other], place.right).wait_recv()
    vecs_ref[...] = functools.reduce(jnp.add, [vring[k] for k in range(vring.shape[0])])[:vecs_ref.shape[0]]
    swap.wait_send()
    for copy in ring:
        copy.wait_send()
    mg.finish()
    hg.finish()
    sc.finish()
    for store in stores:
        store.wait()


def attn_backward(n_tp, scale, dx1, x_in, q_t, k_t, v_t, ctx_t, ctx, lse, wqkv_t, wo, gain, bias, vec):
    batch, rows, width = dx1.shape
    seq = q_t.shape[2]
    any_spec = pl.BlockSpec(memory_space=pl.ANY)
    vm = pl.BlockSpec(memory_space=pltpu.VMEM)
    qkv_rows = wqkv_t.shape[0]
    vrow = pltpu.VMEM((SUB, width), F32)
    return pl.pallas_call(
        functools.partial(attn_kernel, n_tp, scale),
        name='attn_backward',
        out_shape=(jax.ShapeDtypeStruct((batch, rows, width), BF16), jax.ShapeDtypeStruct((qkv_rows, width), F32),
                   jax.ShapeDtypeStruct((LANES, width), F32), jax.ShapeDtypeStruct((1, qkv_rows), F32),
                   jax.ShapeDtypeStruct((6, width), F32)),
        in_specs=[any_spec] * 10 + [vm] * 3,
        out_specs=(any_spec, any_spec, any_spec, vm, vm),
        scratch_shapes=gather_scratch(rows, width) + gather_scratch(rows, width) + scatter_scratch(rows, width) + [
            *[pltpu.VMEM(q_t.shape, BF16)] * 4, *[pltpu.VMEM(ctx.shape, F32)] * 2,
            pltpu.VMEM((qkv_rows, width), BF16), pltpu.VMEM((LANES, width), BF16),
            pltpu.VMEM((batch, qkv_rows, seq), BF16), *[pltpu.VMEM((batch, LANES, seq), F32)] * 2,
            pltpu.VMEM((len(HEADS), rows, LANES), F32),
            pltpu.VMEM((batch, rows, width), F32), pltpu.VMEM((batch, rows, width), BF16),
            pltpu.VMEM((qkv_rows, width), F32), pltpu.VMEM((LANES, width), F32),
            pltpu.VMEM((2, SUB, width), F32), vrow, vrow, pltpu.VMEM((n_tp // CORES, SUB, width), F32),
            pltpu.SemaphoreType.DMA((10,)), pltpu.SemaphoreType.DMA((4,)), pltpu.SemaphoreType.DMA((n_tp + 1,)),
        ],
        compiler_params=pltpu.CompilerParams(collective_id=2, has_side_effects=True, vmem_limit_bytes=VMEM_LIMIT),
    )(dx1, x_in, q_t, k_t, v_t, ctx_t, ctx, lse, wqkv_t, wo, gain.reshape(1, width), bias.reshape(1, width), vec)


def solution(mesh):
    n_tp = mesh.shape['tp']

    def local_backward(x_in, x_mid, d_out, q_saved, k_saved, v_saved, z_saved, ln1_gain, ln1_bias, ln2_gain, ln2_bias, w_qkv, w_proj, w_fc1, w_fc2):
        batch, seq, heads, dim = q_saved.shape
        width = x_in.shape[-1]
        scale = dim ** -0.5

        def feature_rows(a):
            return jnp.transpose(a, (0, 2, 3, 1)).reshape(batch, heads * dim, seq)

        q_t, k_t, v_t = feature_rows(q_saved), feature_rows(k_saved), feature_rows(v_saved)
        wqkv_t = jnp.transpose(w_qkv, (0, 2, 3, 1)).reshape(w_qkv.shape[0] * heads * dim, width)
        wo = w_proj.reshape(heads * dim, width)
        dx1, grad_wfc1, grad_wfc2, ctx_t, ctx, lse, db1, vec = mlp_backward(
            n_tp, scale * LOG2E, d_out, x_mid, z_saved, w_fc1, w_fc2, q_t, k_t, v_t, ln2_gain, ln2_bias)
        grad_x, dwqkv, dwo, dbqkv, grad_vecs = attn_backward(
            n_tp, scale, dx1, x_in, q_t, k_t, v_t, ctx_t, ctx, lse, wqkv_t, wo, ln1_gain, ln1_bias, vec)
        grad_wqkv = jnp.transpose(dwqkv.reshape(-1, heads, dim, width), (0, 3, 1, 2))
        grad_bqkv = dbqkv.reshape(-1, heads, dim)
        grad_wproj = dwo.reshape(heads, dim, width)
        return grad_x, grad_wqkv, grad_bqkv, grad_wproj, grad_wfc1, db1.reshape(-1), grad_wfc2, grad_vecs

    tok_spec = P('dp', 'tp', None)
    head_spec = P('dp', None, 'tp', None)
    in_specs = (tok_spec, tok_spec, tok_spec, head_spec, head_spec, head_spec, P('dp', None, 'tp'),
                P(None), P(None), P(None), P(None),
                P(None, None, 'tp', None), P('tp', None, None), P(None, 'tp'), P('tp', None))
    out_specs = (tok_spec, P('dp', None, 'tp', None), P('dp', 'tp', None), P(('dp', 'tp'), None, None),
                 P('dp', 'tp'), P(('dp', 'tp')), P(('dp', 'tp'), None), P('dp', None))
    return jax.shard_map(local_backward, mesh=mesh, in_specs=in_specs, out_specs=out_specs, check_vma=False)
```

time: 609 us -> 252 us (0.41); the launches traced: 599 us -> 251 us
  matrix products: 319 us -> 0 us
  Pallas kernels: 0 us -> 240 us
  waiting for transfers between devices: 182 us -> 0 us
  other arithmetic: 53.6 us -> 0.8 us
  blocking collectives: 23.5 us -> 0 us
  between operations: 14.7 us -> 0.67 us
    dot_general x12 -> x0, matrix products: 286 us -> none  [the longest x1 82.5 us: attention_grads(): jnp.einsum('bhqk,bqhe->bkhe', grad_scores, q_heads, preferred_element_typ...]
    pallas_call x0 -> x2, Pallas kernels: none -> 240 us  [the longest x1 123 us: attn_backward(): pl.pallas_call(functools.partial(attn_kernel, n_tp, scale), name='attn_ba...]
    reduce_scatter x2 -> x0, waiting for transfers between devices: 94.6 us -> none  [the longest x1 47.4 us: local_backward(): lax.psum_scatter(h1_partial, 'tp', scatter_dimension=1, tiled=True)]
    all_gather x4 -> x0, waiting for transfers between devices: 86.1 us -> none  [the longest x1 52.5 us: local_backward(): dout_full = lax.all_gather(d_out, 'tp', axis=1, tiled=True)]
    convert_element_type x2 -> x0, other arithmetic: 35.9 us -> none  [the longest x1 32.8 us: attention_grads(): probs_low = attn_probs.astype(jnp.bfloat16)]
    sub x1 -> x0, matrix products: 33.5 us -> none  [attention_grads(): attn_probs = jax.nn.softmax(scores, axis=-1)]
    psum x1 -> x0, blocking collectives: 23.5 us -> none  [local_backward(): grad_vecs = lax.psum(vec_partial, 'tp')]
    reduce_sum x8 -> x0, other arithmetic: 13.5 us -> none  [the longest x1 3.87 us: local_backward(): jnp.sum(grad_mid, axis=(0, 1), dtype=jnp.float32)]
  transfers between devices with their start and end apart: 6 -> 0, of which waited for: 4 -> 0; matrix products, arithmetic and copies ran while one was open for 20% -> 0% of each run, Pallas kernels for 0% -> 0%
where the time goes in v1:
time: 252 us; the launch traced here: 251 us
  Pallas kernels  240 us (95%)
  local copies, waits for them, and re-layouts  9.55 us (4%)
    pallas_call x1, Pallas kernels, attn_backward(): pl.pallas_call(functools.partial(attn_kernel, n_tp, scale), name='attn_ba...  123 us
    pallas_call x1, Pallas kernels, mlp_backward(): pl.pallas_call(functools.partial(mlp_kernel, n_tp, scale), name='mlp_back...  116 us
    unnamed x19, local copies, waits for them, and re-layouts  8.89 us

profile of v1, /device:TPU:81, one launch (start us, length us, event | category | flops | bytes accessed | tf_op | source)
XLA Modules:
  0.0 250.8 jit_solution(13144778070051420473)
XLA Ops:
  0.6 116.3 %mlp_backward.1 = (bf16[2,256,1024]{2,1,0:T(8,128)(2,1)}, f32[1024,512]{1,0:T(8,128)}, f32[512,1024]{1,0:T(8,128)}, bf16[2,128,2048]{2,1,0:T(8,128)(2,1)}, f32[2...) custom-call(bf16[2,256,1024]{2,1,0:T(8,128)(2,1)} %dy_hbm.1, ...), custom_call_target="tpu_custom_call" | custom-call | tf_op jit(solution)/shard_map/mlp_backward/pallas_call | solution.py:468
  117.0 123.4 %attn_backward.1 = (bf16[2,256,1024]{2,1,0:T(8,128)(2,1)}, f32[384,1024]{1,0:T(8,128)}, f32[128,1024]{1,0:T(8,128)}, f32[1,384]{1,0:T(1,128)}, f32[6,1024]{1,0:T(8,128)}) custom-call(bf16[2,256,1024]{2,1,0:T(8,128)(2,1)} %get-tuple-element.21.dx1_hbm, bf16[2,256,1024]{2,1,0:T(8,128)(2,1)} %xi_hbm.1, bf16[2,128,2048]{2,1,0:T(8,128)(2,1)} %bitcast.24, ...), custom_call_target="tpu_custom_call" | custom-call | tf_op jit(solution)/shard_map/attn_backward/pallas_call | solution.py:671
  240.4 0.0 copy-start.2
  240.4 0.8 reduce
  241.2 0.7 reshape.69
  241.9 2.3 copy.30
  244.2 0.0 copy-done.2
  244.2 0.0 copy-start.3
  244.2 0.0 copy-start.1
  244.2 1.1 copy.31
  245.3 0.2 copy-done.3
  245.5 0.8 copy.32
  246.3 0.2 copy-done.1
  246.5 0.0 copy-start.5
  246.5 0.0 copy-start
  246.5 1.3 copy.33
  247.8 0.0 copy-done.5
  247.8 0.6 copy.34
  248.4 0.4 copy-done
  248.9 0.0 copy-start.4
  248.9 1.3 copy.35
  250.2 0.0 copy-done.4
  250.2 0.6 copy.36
Async XLA Ops:
  240.4 3.7 %copy-start.2 = (f32[384,1024]{1,0:T(8,128)S(1)}, f32[384,1024]{1,0:T(8,128)}, u32[]{:S(2)}) copy-start(f32[384,1024]{1,0:T(8,128)} %get-tuple-element.27) | copy-start | bytes 4718596
  244.2 1.4 copy-start.3
  244.2 2.3 copy-start.1
  246.5 1.3 copy-start.5
  246.5 2.4 copy-start
  248.9 1.3 copy-start.4

commit v2 on v1

--- a/solution.py
+++ b/solution.py
@@ -542,15 +542,29 @@
         dq = jnp.where(first_head(dq_acc.shape[1:]), dq_acc[0], dq_acc[1]) * scale
         dqkv[b, :LANES, qs] = turn(dq)
 
-    def attend_own(b):
-        mg.wait_partner(b)
-        loop(CORES, lambda p: attend(0, p, b))
+    def attend_own(i):
+        b, p = i // CORES, lax.rem(i, CORES)
+
+        @pl.when(p == 0)
+        def _():
+            mg.wait_partner(b)
+
+        @pl.when(i == len(BATCH) * CORES - 1)
+        def _():
+            mg.relay(0)
+        attend(0, p, b)
 
     def attend_near(b):
-        mg.relay(b)
         for r in (R_RIGHT, R_LEFT):
             mg.wait_shared(r, b)
-        loop(2 * CORES, lambda i: attend(R_RIGHT + 2 * (i // CORES), lax.rem(i, CORES), b))
+
+        def body(i):
+            @pl.when((i == 2 * CORES - 1) & (b == 0))
+            def _():
+                mg.relay(1)
+                hg.start_own(0)
+            attend(R_RIGHT + 2 * (i // CORES), lax.rem(i, CORES), b)
+        loop(2 * CORES, body)
 
     def partial_rows(r, p, b):
         return turn(dqkv[b, :, span(place.block(r, p), rows)])
@@ -562,9 +576,15 @@
             sums[r - 1, b, :, ns] = (mm(lhs, wqkv[:, ns], NN) + p_in[r, b, :, ns].astype(F32)).astype(BF16)
 
     def attend_far(b):
-        mg.relay_far(b)
+        @pl.when(b == 0)
+        def _():
+            mg.relay_far(0)
         mg.wait_shared(R_FAR, b)
         loop(CORES, lambda p: attend(R_FAR, p, b))
+
+        @pl.when(b == 1)
+        def _():
+            sc.send_last(0)
         dqkv[b, LANES:2 * LANES] = (dk_acc[b] * scale).astype(BF16)
         dqkv[b, 2 * LANES:] = dv_acc[b].astype(BF16)
 
@@ -619,17 +639,22 @@
                 vacc[k] += fold8(v)
         loop(rows // STEP, body)
 
-    loop(2, attend_own)
+    def batch(b):
+        @pl.when(b == 1)
+        def _():
+            mg.relay_far(1)
+            hg.start_own(1)
+        attend_near(b)
+        attend_far(b)
+
     normalize(xi, hb, gain_ref, bias_ref)
-    loop(2, attend_near)
-    hg.start_own(0)
-    loop(2, attend_far)
-    hg.start_own(1)
-    loop(2, sc.send_last)
+    loop(len(BATCH) * CORES, attend_own)
+    loop(2, batch)
     hg.relay(0)
     loop(2, dw_own)
     ones = jnp.ones((SUB, dqkv.shape[2]), BF16)
     dbqkv_ref[...] = (mm(ones, dqkv[0], NT) + mm(ones, dqkv[1], NT))[:1]
+    sc.send_last(1)
     hg.relay(1)
     loop(2, dw_near)
     loop(2, back)
@@ -690,6 +715,44 @@
     )(dx1, x_in, q_t, k_t, v_t, ctx_t, ctx, lse, wqkv_t, wo, gain.reshape(1, width), bias.reshape(1, width), vec)
 
 
+def place_results(big, small):
+    pieces = 4
+
+    def kernel(*refs):
+        count, rest = len(big), len(small)
+        src, small_in = refs[:count], refs[count:count + rest]
+        dst, small_out = refs[count + rest:2 * count + rest], refs[2 * count + rest:2 * (count + rest)]
+        bufs, sem_in, sem_out = refs[2 * (count + rest):-2], refs[-2], refs[-1]
+        moves = []
+        for i, buf in enumerate(bufs):
+            step = buf.shape[0] // pieces
+            for j in range(pieces):
+                rs = pl.ds(j * step, step)
+                moves.append((pltpu.make_async_copy(src[i].at[rs], buf.at[rs], sem_in.at[i, j]),
+                              pltpu.make_async_copy(buf.at[rs], dst[i].at[rs], sem_out.at[i, j])))
+        for fetch, _ in moves:
+            fetch.start()
+        for ref_in, ref_out in zip(small_in, small_out):
+            ref_out[...] = ref_in[...]
+        for fetch, put in moves:
+            fetch.wait()
+            put.start()
+        for _, put in moves:
+            put.wait()
+
+    any_spec = pl.BlockSpec(memory_space=pl.ANY)
+    vm = pl.BlockSpec(memory_space=pltpu.VMEM)
+    return pl.pallas_call(
+        kernel,
+        name='place_results',
+        out_shape=[jax.ShapeDtypeStruct(v.shape, v.dtype) for v in (*big, *small)],
+        in_specs=[any_spec] * len(big) + [vm] * len(small),
+        out_specs=[any_spec] * len(big) + [vm] * len(small),
+        scratch_shapes=[pltpu.VMEM(v.shape, v.dtype) for v in big] + [pltpu.SemaphoreType.DMA((len(big), pieces))] * 2,
+        compiler_params=pltpu.CompilerParams(vmem_limit_bytes=VMEM_LIMIT),
+    )(*big, *small)
+
+
 def solution(mesh):
     n_tp = mesh.shape['tp']
 
@@ -708,6 +771,9 @@
             n_tp, scale * LOG2E, d_out, x_mid, z_saved, w_fc1, w_fc2, q_t, k_t, v_t, ln2_gain, ln2_bias)
         grad_x, dwqkv, dwo, dbqkv, grad_vecs = attn_backward(
             n_tp, scale, dx1, x_in, q_t, k_t, v_t, ctx_t, ctx, lse, wqkv_t, wo, ln1_gain, ln1_bias, vec)
+        grad_x, grad_wfc1, grad_wfc2, dwqkv, dwo, db1, dbqkv, grad_vecs = place_results(
+            (grad_x.reshape(batch * x_in.shape[1], width), grad_wfc1, grad_wfc2, dwqkv, dwo), (db1, dbqkv, grad_vecs))
+        grad_x = grad_x.reshape(x_in.shape)
         grad_wqkv = jnp.transpose(dwqkv.reshape(-1, heads, dim, width), (0, 3, 1, 2))
         grad_bqkv = dbqkv.reshape(-1, heads, dim)
         grad_wproj = dwo.reshape(heads, dim, width)

time: 252 us -> 237 us (0.940)
  local copies, waits for them, and re-layouts: 9.55 us -> 0.66 us
  Pallas kernels: 240 us -> 235 us
    pallas_call x1, Pallas kernels: 123 us -> 112 us  [attn_backward(): pl.pallas_call(functools.partial(attn_kernel, n_tp, scale), name='attn_ba...]
    unnamed x19 -> x0, local copies, waits for them, and re-layouts: 8.89 us -> none
    pallas_call x0 -> x1, Pallas kernels: none -> 7.26 us  [place_results(): pl.pallas_call(kernel, name='place_results', out_shape=[jax.ShapeDtypeStr...]
where the time goes in v2:
time: 237 us
  Pallas kernels  235 us (99%)
    pallas_call x1, Pallas kernels, mlp_backward(): pl.pallas_call(functools.partial(mlp_kernel, n_tp, scale), name='mlp_back...  116 us
    pallas_call x1, Pallas kernels, attn_backward(): pl.pallas_call(functools.partial(attn_kernel, n_tp, scale), name='attn_ba...  112 us
    pallas_call x1, Pallas kernels, place_results(): pl.pallas_call(kernel, name='place_results', out_shape=[jax.ShapeDtypeStr...  7.26 us

profile of v2, /device:TPU:81, one launch (start us, length us, event | category | flops | bytes accessed | tf_op | source)
XLA Modules:
  0.0 237.1 jit_solution(17453141470477057496)
XLA Ops:
  0.6 116.3 %mlp_backward.1 = (bf16[2,256,1024]{2,1,0:T(8,128)(2,1)}, f32[1024,512]{1,0:T(8,128)}, f32[512,1024]{1,0:T(8,128)}, bf16[2,128,2048]{2,1,0:T(8,128)(2,1)}, f32[2...) custom-call(bf16[2,256,1024]{2,1,0:T(8,128)(2,1)} %dy_hbm.1, ...), custom_call_target="tpu_custom_call" | custom-call | tf_op jit(solution)/shard_map/mlp_backward/pallas_call | solution.py:468
  117.0 111.5 %attn_backward.1 = (bf16[2,256,1024]{2,1,0:T(8,128)(2,1)}, f32[384,1024]{1,0:T(8,128)}, f32[128,1024]{1,0:T(8,128)}, f32[1,384]{1,0:T(1,128)}, f32[6,1024]{1,0:T(8,128)}) custom-call(bf16[2,256,1024]{2,1,0:T(8,128)(2,1)} %get-tuple-element.29.dx1_hbm, bf16[2,256,1024]{2,1,0:T(8,128)(2,1)} %xi_hbm.1, bf16[2,128,2048]{2,1,0:T(8,128)(2,1)} %bitcast.26, ...), custom_call_target="tpu_custom_call" | custom-call | tf_op jit(solution)/shard_map/attn_backward/pallas_call | solution.py:696
  228.5 7.3 %place_results.1 = (bf16[512,1024]{1,0:T(8,128)(2,1)}, f32[1024,512]{1,0:T(8,128)}, f32[512,1024]{1,0:T(8,128)}, f32[384,1024]{1,0:T(8,128)}, f32[128,1024]{1,0:...) custom-call(bf16[512,1024]{1,0:T(8,128)(2,1)} %bitcast.32, ...), custom_call_target="tpu_custom_call" | custom-call | tf_op jit(solution)/shard_map/place_results/pallas_call | solution.py:745
  235.8 0.7 reduce
  236.5 0.7 reshape.77

commit v3 on v2

--- a/solution.py
+++ b/solution.py
@@ -78,15 +78,13 @@
     return inv_std * (centered - x_hat * jnp.mean(grad_hat * x_hat, axis=-1, keepdims=True))
 
 
-def normalize(src, dst, gain, bias):
-    per = src.shape[1] // STEP
-
+def normalize(src, dst, gain, bias, b):
     def body(i):
-        b, rs = i // per, span(lax.rem(i, per), STEP)
+        rs = span(i, STEP)
         x_hat, _ = ln_stats(src[b, rs].astype(F32))
         dst[0, b, rs] = (x_hat * gain[...] + bias[...]).astype(BF16)
 
-    loop(len(BATCH) * per, body)
+    loop(src.shape[1] // STEP, body)
 
 
 def start_copies(pairs, sems):
@@ -175,11 +173,21 @@
     def wait_partner(self, b):
         self.to_partner(b).wait_recv()
 
-    def finish(self):
-        for b in BATCH:
-            for copy in (self.to_partner(b), self.to_right(b), self.to_left(b), self.fwd_right(b), self.fwd_left(b),
-                         *(self.share(r, b) for r in RING)):
-                copy.wait_send()
+    def drain_own(self, b):
+        for copy in (self.to_partner, self.to_right, self.to_left):
+            copy(b).wait_send()
+
+    def drain_near(self, b):
+        for copy in (self.fwd_right(b), self.fwd_left(b), self.share(R_RIGHT, b), self.share(R_LEFT, b)):
+            copy.wait_send()
+
+    def drain_far(self, b):
+        self.share(R_FAR, b).wait_send()
+
+    def drain(self, b):
+        self.drain_own(b)
+        self.drain_near(b)
+        self.drain_far(b)
 
 
 class Scatter:
@@ -247,13 +255,11 @@
 def scatter_scratch(rows, width):
     def buf(*lead):
         return pltpu.VMEM((*lead, len(BATCH), rows, width), BF16)
-    return [buf(4), buf(4), buf(3), buf(2), pltpu.VMEM((2, len(BATCH), rows // 2, width), BF16),
-            pltpu.SemaphoreType.DMA((10, 2)), pltpu.SemaphoreType.DMA((10, 2))]
-
-
-def gather_scratch(rows, width):
-    return [pltpu.VMEM((SLOT_END, len(BATCH), rows, width), BF16),
-            pltpu.SemaphoreType.DMA((SLOT_END, 2)), pltpu.SemaphoreType.DMA((SLOT_END + 1, 2))]
+    return [buf(4), buf(4), buf(3), buf(2), pltpu.VMEM((2, len(BATCH), rows // 2, width), BF16)]
+
+
+def copy_sems(*counts):
+    return [pltpu.SemaphoreType.DMA((count, len(BATCH))) for count in counts]
 
 
 def first_head(shape):
@@ -312,40 +318,53 @@
     first = first_head(m_buf.shape[1:])
     out = jnp.where(first, m_buf[0], m_buf[1])
     ctx[b, blk] = out
-    lse[b, blk] = jnp.where(first, *l_col)
+    lse_t = jnp.transpose(jnp.where(first, *l_col))
+    for h in HEADS:
+        top = h * (LANES // len(HEADS))
+        lse[b, blk, h:h + 1] = lse_t[top:top + 1]
     ctx_t[b, :, qs] = turn(out)
 
 
-def mlp_kernel(n_tp, scale, dy_hbm, xm_hbm, z_hbm, w1_hbm, w2_hbm, q_hbm, k_hbm, v_hbm, gain_ref, bias_ref,
-               dx1_hbm, dw1_hbm, dw2_hbm, ctxt_hbm, ctx_hbm, lse_hbm, db1_ref, vec_ref,
-               dyb, dy_ss, dy_rs, hb, h_ss, h_rs, p_out, p_in, sums, fin, transit, rs_ss, rs_rs,
-               z, w1, w2, dw1, dw2, own, xm, db1, q_t, k_t, v_t, ctx_t, ctx, lse, s_buf, m_buf, lsem):
+def backward_kernel(n_tp, scale, dy_hbm, xm_hbm, z_hbm, w1_hbm, w2_hbm, q_hbm, k_hbm, v_hbm, xi_hbm, wqkv_hbm, wo_hbm,
+                    gain2_ref, bias2_ref, gain1_ref, bias1_ref,
+                    dx_hbm, dw1_hbm, dw2_hbm, dwqkv_hbm, dwo_hbm, db1_ref, dbqkv_ref, vecs_ref,
+                    tok, hb, p_out, p_in, sums, fin, transit,
+                    z, w1, w2, dw1, dw2, own, xm, xi, db1, q_t, k_t, v_t, ctx_t, ctx, lse, acc, head_acc,
+                    wqkv, wo, dqkv, dwqkv, dwo, vacc, vsend, vrecv, vring,
+                    dy_ss, dy_rs, h2_ss, h2_rs, dx_ss, dx_rs, h1_ss, h1_rs, rs2_ss, rs2_rs, rs1_ss, rs1_rs,
+                    lsem, v_ss, v_rs, credit):
     place = Place(n_tp)
     rows, width = dy_hbm.shape[1:]
     units = w2.shape[0]
     blocks = ctx.shape[1]
-    place.enter((place.partner, place.right, place.left))
-    dyg = Gather(place, dy_hbm, dyb, dy_ss, dy_rs)
-    hg = Gather(place, hb.at[0], hb, h_ss, h_rs)
-    sc = Scatter(place, p_out, p_in, sums, fin, transit, rs_ss, rs_rs)
+    neighbours = (place.partner, place.right, place.left)
+    place.enter((*neighbours, place.far))
+    dyg = Gather(place, dy_hbm, tok, dy_ss, dy_rs)
+    mg = Gather(place, tok.at[0], tok, dx_ss, dx_rs)
+    h2g = Gather(place, hb.at[0], hb, h2_ss, h2_rs)
+    h1g = Gather(place, hb.at[0], hb, h1_ss, h1_rs)
+    sc2 = Scatter(place, p_out, p_in, sums, fin, transit, rs2_ss, rs2_rs)
+    sc1 = Scatter(place, p_out, p_in, sums, fin, transit, rs1_ss, rs1_rs)
     for b in BATCH:
         dyg.start_own(b)
-    loads = start_copies(((xm_hbm, xm), (dy_hbm, dyb.at[0]), (w2_hbm, w2), (z_hbm, z), (w1_hbm, w1),
-                          (q_hbm, q_t), (k_hbm, k_t), (v_hbm, v_t)), lsem)
-    clear(dw1, dw2, db1, vec_ref)
+    loads = start_copies(((xm_hbm, xm), (dy_hbm, tok.at[0]), (w2_hbm, w2), (z_hbm, z), (w1_hbm, w1),
+                          (q_hbm, q_t), (k_hbm, k_t), (v_hbm, v_t), (wo_hbm, wo), (wqkv_hbm, wqkv), (xi_hbm, xi)), lsem)
+    clear(dw1, dw2, db1, vacc, vsend, dwqkv, dwo, lse)
     loads[0].wait()
-    normalize(xm, hb, gain_ref, bias_ref)
+    loop(2, functools.partial(normalize, xm, hb, gain2_ref, bias2_ref))
     for load in loads[1:]:
         load.wait()
-
-    def attend(lo, count):
+    exp_scale = scale * LOG2E
+    dim = LANES // len(HEADS)
+
+    def recall(lo, count):
         def body(i):
             i = lo + i
-            attn_fwd_block(i // blocks, lax.rem(i, blocks), q_t, k_t, v_t, ctx_t, ctx, lse, s_buf, m_buf, scale)
+            attn_fwd_block(i // blocks, lax.rem(i, blocks), q_t, k_t, v_t, ctx_t, ctx, lse, acc, head_acc, exp_scale)
         loop(count, body)
 
     def pre_piece(r, p, b):
-        dy, blk = dyb[CORES * r + p, b], place.block(r, p)
+        dy, blk = tok[CORES * r + p, b], place.block(r, p)
         for fs in columns(units):
             act = mm(dy, w2[fs, :], NT)
             zf = z[b, blk, :, fs].astype(F32)
@@ -363,9 +382,9 @@
         dz = pre_piece(r, 1, b)
         for ns in columns(width):
             p_out[r, b, :, ns] = mm(dz, w1[ns, :], NT).astype(BF16)
-        sc.to_partner(r, b).start()
+        sc2.to_partner(r, b).start()
         dz = pre_piece(r, 0, b)
-        sc.to_partner(r, b).wait_recv()
+        sc2.to_partner(r, b).wait_recv()
         for ns in columns(width):
             put(ns, mm(dz, w1[ns, :], NT) + p_in[r, b, :, ns].astype(F32))
 
@@ -386,14 +405,15 @@
     def near_body(b):
         dyg.relay(b)
         loop(2, lambda i: pair_out(R_RIGHT + 2 * i, b))
-        sc.send_near(b)
-        attend(2 * b, 2)
+        sc2.send_near(b)
+        recall(2 * b, 2)
 
     def far_body(b):
         dyg.relay_far(b)
         pair_out(R_FAR, b)
-        sc.send_far(b)
-        hg.start_own(b)
+        dyg.drain_far(b)
+        sc2.send_far(b)
+        h2g.start_own(b)
 
     def dw1_pair(r, b):
         def body(p):
@@ -401,116 +421,50 @@
         loop(CORES, body)
 
     def dw1_own(b):
-        hg.wait_partner(b)
+        h2g.wait_partner(b)
         dw1_pair(0, b)
 
     def dw1_near(b):
         def body(i):
             r = R_RIGHT + 2 * i
-            hg.wait_shared(r, b)
+            h2g.wait_shared(r, b)
             dw1_pair(r, b)
         loop(2, body)
 
     def dw1_far(b):
-        hg.relay_far(b)
-        hg.wait_shared(R_FAR, b)
+        h2g.relay_far(b)
+        h2g.wait_shared(R_FAR, b)
         dw1_pair(R_FAR, b)
-
-    def back(b):
-        sc.wait_final(b)
+        h2g.drain(b)
+        for peer in neighbours:
+            pl.semaphore_signal(credit.at[b], inc=1, device_id={'tp': peer}, device_id_type=MESH)
+        normalize(xi, hb, gain1_ref, bias1_ref, b)
+
+    def start_h1(b):
+        pl.semaphore_wait(credit.at[b], len(neighbours))
+        h1g.start_own(b)
+
+    def back2(b):
+        sc2.wait_final(b)
 
         def body(i):
             rs = span(i, STEP)
-            grad = sc.total(own, b, rs)
+            grad = sc2.total(own, b, rs)
             x_hat, inv_std = ln_stats(xm[b, rs].astype(F32))
-            dyf = dyb[0, b, rs].astype(F32)
-            dx1 = (dyf + ln_bwd(grad, x_hat, inv_std, gain_ref[...])).astype(BF16)
-            xm[b, rs] = dx1
+            dyf = tok[0, b, rs].astype(F32)
+            dx1 = (dyf + ln_bwd(grad, x_hat, inv_std, gain2_ref[...])).astype(BF16)
+            tok[0, b, rs] = dx1
             for k, v in enumerate((grad * x_hat, grad, dx1.astype(F32), dyf)):
-                vec_ref[k] += fold8(v)
+                vacc[2 + k] += fold8(v)
         loop(rows // STEP, body)
-
-    loop(2, own_body)
-    loop(2, near_body)
-    loop(2, far_body)
-    rest = 2 * blocks - 4
-    attend(4, rest)
-    ctx_stores = start_copies(((ctx_t, ctxt_hbm), (ctx, ctx_hbm), (lse, lse_hbm)), lsem)
-    loop(2, sc.send_last)
-    hg.relay(0)
-    loop(2, dw1_own)
-    hg.relay(1)
-    loop(2, dw1_near)
-    loop(2, back)
-    for store in ctx_stores:
-        store.wait()
-    stores = start_copies(((xm, dx1_hbm), (dw2, dw2_hbm)), lsem)
-    db1_ref[...] = jnp.sum(db1[...], axis=0, keepdims=True)
-    loop(2, dw1_far)
-    for store in stores:
-        store.wait()
-    stores = start_copies(((dw1, dw1_hbm),), lsem)
-    dyg.finish()
-    hg.finish()
-    sc.finish()
-    stores[0].wait()
-
-
-def mlp_backward(n_tp, scale, d_out, x_mid, z, w1, w2, q_t, k_t, v_t, gain, bias):
-    batch, rows, width = d_out.shape
-    units = w2.shape[0]
-    seq = q_t.shape[2]
-    blocks = seq // rows
-    any_spec = pl.BlockSpec(memory_space=pl.ANY)
-    vm = pl.BlockSpec(memory_space=pltpu.VMEM)
-    heads_t = (batch, LANES, seq)
-    per_row = (batch, blocks, rows, LANES)
-    return pl.pallas_call(
-        functools.partial(mlp_kernel, n_tp, scale),
-        name='mlp_backward',
-        out_shape=(jax.ShapeDtypeStruct((batch, rows, width), BF16), jax.ShapeDtypeStruct((width, units), F32),
-                   jax.ShapeDtypeStruct((units, width), F32), jax.ShapeDtypeStruct(heads_t, BF16),
-                   jax.ShapeDtypeStruct(per_row, F32), jax.ShapeDtypeStruct(per_row, F32),
-                   jax.ShapeDtypeStruct((1, units), F32), jax.ShapeDtypeStruct((4, SUB, width), F32)),
-        in_specs=[any_spec] * 8 + [vm] * 2,
-        out_specs=(*[any_spec] * 6, vm, vm),
-        scratch_shapes=gather_scratch(rows, width) + gather_scratch(rows, width) + scatter_scratch(rows, width) + [
-            pltpu.VMEM((batch, blocks, rows, units), BF16),
-            pltpu.VMEM((width, units), BF16), pltpu.VMEM((units, width), BF16),
-            pltpu.VMEM((width, units), F32), pltpu.VMEM((units, width), F32),
-            pltpu.VMEM((batch, rows, width), F32), pltpu.VMEM((batch, rows, width), BF16),
-            pltpu.VMEM((SUB, units), F32), *[pltpu.VMEM(heads_t, BF16)] * 4, *[pltpu.VMEM(per_row, F32)] * 2,
-            pltpu.VMEM((len(HEADS), rows, seq), F32), pltpu.VMEM((len(HEADS), rows, LANES), F32),
-            pltpu.SemaphoreType.DMA((8,)),
-        ],
-        compiler_params=pltpu.CompilerParams(collective_id=1, has_side_effects=True, vmem_limit_bytes=VMEM_LIMIT),
-    )(d_out, x_mid, z.reshape(batch, blocks, rows, units), w1, w2, q_t, k_t, v_t, gain.reshape(1, width), bias.reshape(1, width))
-
-
-def attn_kernel(n_tp, scale, dx1_hbm, xi_hbm, q_hbm, k_hbm, v_hbm, ctxt_hbm, ctx_hbm, lse_hbm, wqkv_hbm, wo_hbm,
-                gain_ref, bias_ref, vec_in,
-                dx_hbm, dwqkv_hbm, dwo_hbm, dbqkv_ref, vecs_ref,
-                mb, m_ss, m_rs, hb, h_ss, h_rs, p_out, p_in, sums, fin, transit, rs_ss, rs_rs,
-                q_t, k_t, v_t, ctx_t, ctx, lse, wqkv, wo, dqkv, dk_acc, dv_acc, dq_acc,
-                own, xi, dwqkv, dwo, vacc, vsend, vrecv, vring, lsem, v_ss, v_rs):
-    place = Place(n_tp)
-    rows, width = dx1_hbm.shape[1:]
-    place.enter((place.partner, place.right, place.left, place.far))
-    mg = Gather(place, dx1_hbm, mb, m_ss, m_rs)
-    hg = Gather(place, hb.at[0], hb, h_ss, h_rs)
-    sc = Scatter(place, p_out, p_in, sums, fin, transit, rs_ss, rs_rs)
-    for b in BATCH:
         mg.start_own(b)
-    loads = start_copies(((dx1_hbm, mb.at[0]), (wo_hbm, wo), (q_hbm, q_t), (k_hbm, k_t), (v_hbm, v_t), (ctx_hbm, ctx),
-                          (lse_hbm, lse), (ctxt_hbm, ctx_t), (wqkv_hbm, wqkv), (xi_hbm, xi)), lsem)
-    clear(dwqkv, dwo, dk_acc, dv_acc, vacc, vsend)
-    for load in loads:
-        load.wait()
-    exp_scale = scale * LOG2E
-    dim = LANES // len(HEADS)
+
+    def last2(b):
+        dyg.drain_near(b)
+        sc2.send_last(b)
 
     def attend(r, p, b):
-        mid, blk = mb[CORES * r + p, b], place.block(r, p)
+        mid, blk = tok[CORES * r + p, b], place.block(r, p)
         qs = span(blk, rows)
         dwo[...] += mm(ctx_t[b, :, qs], mid, NN)
         dctx = mm(mid, wo[...], NT).astype(BF16)
@@ -518,28 +472,28 @@
         qt = q_t[b, :, qs]
         q_h, d_h = split_heads(turn(qt)), split_heads(dctx)
         delta = [jnp.sum(v, axis=-1, keepdims=True) for v in split_heads(dctx.astype(F32) * ctx[b, blk])]
-        lse_v = lse[b, blk]
-        l_col = [lse_v[:, h * dim:h * dim + 1] for h in HEADS]
+        lse_v = jnp.transpose(lse[b, blk])
+        l_col = [lse_v[:, h:h + 1] for h in HEADS]
         last = blk // (TK // rows)
-        clear(dq_acc)
+        clear(head_acc)
 
         def tile(j, masked=False):
             ks = span(j, TK)
             kk, vv = k_t[b, :, ks], v_t[b, :, ks]
             for h in HEADS:
-                hs = pl.ds(h * dim, dim)
+                hs = pl.ds(pl.multiple_of(b * LANES + h * dim, dim), dim)
                 top = slice(h * dim, (h + 1) * dim)
                 prob = jnp.exp2(mm(q_h[h], kk, NN) * exp_scale - l_col[h])
                 if masked:
                     prob = jnp.where(visible(blk, j, rows), prob, 0.0)
                 ds = (prob * (mm(d_h[h], vv, NN) - delta[h])).astype(BF16)
-                dq_acc[h] += mm(ds, kk, NT)
-                dk_acc[b, hs, ks] += mm(qt[top], ds, NN)
-                dv_acc[b, hs, ks] += mm(dctx_t[top], prob.astype(BF16), NN)
+                head_acc[h] += mm(ds, kk, NT)
+                acc[0, hs, ks] += mm(qt[top], ds, NN)
+                acc[1, hs, ks] += mm(dctx_t[top], prob.astype(BF16), NN)
 
         tile(last, True)
         loop(last, tile)
-        dq = jnp.where(first_head(dq_acc.shape[1:]), dq_acc[0], dq_acc[1]) * scale
+        dq = jnp.where(first_head(head_acc.shape[1:]), head_acc[0], head_acc[1]) * scale
         dqkv[b, :LANES, qs] = turn(dq)
 
     def attend_own(i):
@@ -548,10 +502,6 @@
         @pl.when(p == 0)
         def _():
             mg.wait_partner(b)
-
-        @pl.when(i == len(BATCH) * CORES - 1)
-        def _():
-            mg.relay(0)
         attend(0, p, b)
 
     def attend_near(b):
@@ -562,7 +512,7 @@
             @pl.when((i == 2 * CORES - 1) & (b == 0))
             def _():
                 mg.relay(1)
-                hg.start_own(0)
+                start_h1(0)
             attend(R_RIGHT + 2 * (i // CORES), lax.rem(i, CORES), b)
         loop(2 * CORES, body)
 
@@ -571,7 +521,7 @@
 
     def reduce_out(r, b):
         lhs = partial_rows(r, 0, b)
-        sc.to_partner(r, b).wait_recv()
+        sc1.to_partner(r, b).wait_recv()
         for ns in columns(width):
             sums[r - 1, b, :, ns] = (mm(lhs, wqkv[:, ns], NN) + p_in[r, b, :, ns].astype(F32)).astype(BF16)
 
@@ -584,24 +534,25 @@
 
         @pl.when(b == 1)
         def _():
-            sc.send_last(0)
-        dqkv[b, LANES:2 * LANES] = (dk_acc[b] * scale).astype(BF16)
-        dqkv[b, 2 * LANES:] = dv_acc[b].astype(BF16)
+            sc1.send_last(0)
+        mine = span(b, LANES)
+        dqkv[b, LANES:2 * LANES] = (acc[0, mine] * scale).astype(BF16)
+        dqkv[b, 2 * LANES:] = acc[1, mine].astype(BF16)
 
         def to_partner(i):
             r = lax.rem(R_FAR + i, place.chips)
             lhs = partial_rows(r, 1, b)
             for ns in columns(width):
                 p_out[r, b, :, ns] = mm(lhs, wqkv[:, ns], NN).astype(BF16)
-            sc.to_partner(r, b).start()
+            sc1.to_partner(r, b).start()
 
         loop(place.chips, to_partner)
         reduce_out(R_FAR, b)
-        sc.send_far(b)
+        sc1.send_far(b)
         loop(2, lambda i: reduce_out(R_RIGHT + 2 * i, b))
-        sc.send_near(b)
+        sc1.send_near(b)
         lhs = partial_rows(0, 0, b)
-        sc.to_partner(0, b).wait_recv()
+        sc1.to_partner(0, b).wait_recv()
         for ns in columns(width):
             own[b, :, ns] = mm(lhs, wqkv[:, ns], NN) + p_in[0, b, :, ns].astype(F32)
 
@@ -611,57 +562,73 @@
         loop(CORES, body)
 
     def dw_own(b):
-        hg.wait_partner(b)
+        h1g.wait_partner(b)
         dw_pair(0, b)
 
     def dw_near(b):
         def body(i):
             r = R_RIGHT + 2 * i
-            hg.wait_shared(r, b)
+            h1g.wait_shared(r, b)
             dw_pair(r, b)
         loop(2, body)
 
     def dw_far(b):
-        hg.relay_far(b)
-        hg.wait_shared(R_FAR, b)
+        h1g.relay_far(b)
+        h1g.wait_shared(R_FAR, b)
         dw_pair(R_FAR, b)
 
-    def back(b):
-        sc.wait_final(b)
+    def back1(b):
+        sc1.wait_final(b)
 
         def body(i):
             rs = span(i, STEP)
-            grad = sc.total(own, b, rs)
+            grad = sc1.total(own, b, rs)
             x_hat, inv_std = ln_stats(xi[b, rs].astype(F32))
-            dx = (mb[0, b, rs].astype(F32) + ln_bwd(grad, x_hat, inv_std, gain_ref[...])).astype(BF16)
+            dx = (tok[0, b, rs].astype(F32) + ln_bwd(grad, x_hat, inv_std, gain1_ref[...])).astype(BF16)
             xi[b, rs] = dx
             for k, v in enumerate((grad * x_hat, grad)):
                 vacc[k] += fold8(v)
         loop(rows // STEP, body)
 
+    loop(2, own_body)
+    loop(2, near_body)
+    loop(2, far_body)
+    recall(4, 2 * blocks - 4)
+    clear(acc)
+    loop(2, last2)
+    h2g.relay(0)
+    loop(2, dw1_own)
+    h2g.relay(1)
+    loop(2, dw1_near)
+    loop(2, back2)
+    stores = start_copies(((dw2, dw2_hbm),), lsem)
+    sc2.finish()
+    loop(len(BATCH) * CORES, attend_own)
+    loop(2, dw1_far)
+    stores += start_copies(((dw1, dw1_hbm),), lsem.at[pl.ds(1, 1)])
+    db1_ref[...] = jnp.sum(db1[...], axis=0, keepdims=True)
+    mg.relay(0)
+
     def batch(b):
         @pl.when(b == 1)
         def _():
             mg.relay_far(1)
-            hg.start_own(1)
+            start_h1(1)
         attend_near(b)
         attend_far(b)
 
-    normalize(xi, hb, gain_ref, bias_ref)
-    loop(len(BATCH) * CORES, attend_own)
     loop(2, batch)
-    hg.relay(0)
+    h1g.relay(0)
     loop(2, dw_own)
     ones = jnp.ones((SUB, dqkv.shape[2]), BF16)
     dbqkv_ref[...] = (mm(ones, dqkv[0], NT) + mm(ones, dqkv[1], NT))[:1]
-    sc.send_last(1)
-    hg.relay(1)
+    sc1.send_last(1)
+    h1g.relay(1)
     loop(2, dw_near)
-    loop(2, back)
-    stores = start_copies(((xi, dx_hbm), (dwo, dwo_hbm)), lsem)
-    rows_in = [vacc[k] for k in range(vacc.shape[0])] + [vec_in[k] for k in range(vec_in.shape[0])]
-    for k, v in enumerate(rows_in):
-        vsend[k:k + 1] = jnp.sum(v, axis=0, keepdims=True)
+    loop(2, back1)
+    stores += start_copies(((xi, dx_hbm), (dwo, dwo_hbm)), lsem.at[pl.ds(2, 2)])
+    for k in range(vacc.shape[0]):
+        vsend[k:k + 1] = jnp.sum(vacc[k], axis=0, keepdims=True)
     swap = remote(vsend, vrecv, v_ss.at[0], v_rs.at[n_tp], place.partner)
     swap.start()
     swap.wait_recv()
@@ -671,7 +638,7 @@
     for copy in ring:
         copy.start()
     loop(2, dw_far)
-    stores += start_copies(((dwqkv, dwqkv_hbm),), lsem.at[pl.ds(2, 1)])
+    stores += start_copies(((dwqkv, dwqkv_hbm),), lsem.at[pl.ds(4, 1)])
     for r in RING:
         other = lax.rem(place.x + r, place.chips)
         remote(vring.at[other], vring.at[other], v_ss.at[r], v_rs.at[other], place.right).wait_recv()
@@ -679,40 +646,55 @@
     swap.wait_send()
     for copy in ring:
         copy.wait_send()
-    mg.finish()
-    hg.finish()
-    sc.finish()
+    for b in BATCH:
+        dyg.drain_own(b)
+        mg.drain(b)
+        h1g.drain(b)
+    sc1.finish()
     for store in stores:
         store.wait()
 
 
-def attn_backward(n_tp, scale, dx1, x_in, q_t, k_t, v_t, ctx_t, ctx, lse, wqkv_t, wo, gain, bias, vec):
-    batch, rows, width = dx1.shape
+def backward(n_tp, scale, d_out, x_mid, z, w1, w2, q_t, k_t, v_t, x_in, wqkv_t, wo, gain2, bias2, gain1, bias1):
+    batch, rows, width = d_out.shape
+    units = w2.shape[0]
     seq = q_t.shape[2]
+    blocks = seq // rows
+    qkv_rows = wqkv_t.shape[0]
     any_spec = pl.BlockSpec(memory_space=pl.ANY)
     vm = pl.BlockSpec(memory_space=pltpu.VMEM)
-    qkv_rows = wqkv_t.shape[0]
-    vrow = pltpu.VMEM((SUB, width), F32)
+    slots = pltpu.VMEM((SLOT_END, batch, rows, width), BF16)
+    row = pltpu.VMEM((SUB, width), F32)
+
+    def shape(*dims):
+        return jax.ShapeDtypeStruct(dims, F32)
+
     return pl.pallas_call(
-        functools.partial(attn_kernel, n_tp, scale),
-        name='attn_backward',
-        out_shape=(jax.ShapeDtypeStruct((batch, rows, width), BF16), jax.ShapeDtypeStruct((qkv_rows, width), F32),
-                   jax.ShapeDtypeStruct((LANES, width), F32), jax.ShapeDtypeStruct((1, qkv_rows), F32),
-                   jax.ShapeDtypeStruct((6, width), F32)),
-        in_specs=[any_spec] * 10 + [vm] * 3,
-        out_specs=(any_spec, any_spec, any_spec, vm, vm),
-        scratch_shapes=gather_scratch(rows, width) + gather_scratch(rows, width) + scatter_scratch(rows, width) + [
-            *[pltpu.VMEM(q_t.shape, BF16)] * 4, *[pltpu.VMEM(ctx.shape, F32)] * 2,
-            pltpu.VMEM((qkv_rows, width), BF16), pltpu.VMEM((LANES, width), BF16),
-            pltpu.VMEM((batch, qkv_rows, seq), BF16), *[pltpu.VMEM((batch, LANES, seq), F32)] * 2,
-            pltpu.VMEM((len(HEADS), rows, LANES), F32),
-            pltpu.VMEM((batch, rows, width), F32), pltpu.VMEM((batch, rows, width), BF16),
+        functools.partial(backward_kernel, n_tp, scale),
+        name='layer_backward',
+        out_shape=(jax.ShapeDtypeStruct((batch, rows, width), BF16), shape(width, units), shape(units, width),
+                   shape(qkv_rows, width), shape(LANES, width), shape(1, units), shape(1, qkv_rows), shape(6, width)),
+        in_specs=[any_spec] * 11 + [vm] * 4,
+        out_specs=(*[any_spec] * 5, vm, vm, vm),
+        scratch_shapes=[
+            slots, slots, *scatter_scratch(rows, width),
+            pltpu.VMEM((batch, blocks, rows, units), BF16),
+            pltpu.VMEM((width, units), BF16), pltpu.VMEM((units, width), BF16),
+            pltpu.VMEM((width, units), F32), pltpu.VMEM((units, width), F32),
+            pltpu.VMEM((batch, rows, width), F32), *[pltpu.VMEM((batch, rows, width), BF16)] * 2,
+            pltpu.VMEM((SUB, units), F32), *[pltpu.VMEM((batch, LANES, seq), BF16)] * 4,
+            pltpu.VMEM((batch, blocks, rows, LANES), F32), pltpu.VMEM((batch, blocks, SUB, rows), F32),
+            pltpu.VMEM((len(HEADS), rows, seq), F32), pltpu.VMEM((len(HEADS), rows, LANES), F32),
+            pltpu.VMEM((qkv_rows, width), BF16), pltpu.VMEM((LANES, width), BF16), pltpu.VMEM((batch, qkv_rows, seq), BF16),
             pltpu.VMEM((qkv_rows, width), F32), pltpu.VMEM((LANES, width), F32),
-            pltpu.VMEM((2, SUB, width), F32), vrow, vrow, pltpu.VMEM((n_tp // CORES, SUB, width), F32),
-            pltpu.SemaphoreType.DMA((10,)), pltpu.SemaphoreType.DMA((4,)), pltpu.SemaphoreType.DMA((n_tp + 1,)),
+            pltpu.VMEM((6, SUB, width), F32), row, row, pltpu.VMEM((n_tp // CORES, SUB, width), F32),
+            *copy_sems(*[SLOT_END, SLOT_END + 1] * 4, *[10] * 4),
+            pltpu.SemaphoreType.DMA((11,)), pltpu.SemaphoreType.DMA((4,)), pltpu.SemaphoreType.DMA((n_tp + 1,)),
+            pltpu.SemaphoreType.REGULAR((batch,)),
         ],
-        compiler_params=pltpu.CompilerParams(collective_id=2, has_side_effects=True, vmem_limit_bytes=VMEM_LIMIT),
-    )(dx1, x_in, q_t, k_t, v_t, ctx_t, ctx, lse, wqkv_t, wo, gain.reshape(1, width), bias.reshape(1, width), vec)
+        compiler_params=pltpu.CompilerParams(collective_id=1, has_side_effects=True, vmem_limit_bytes=VMEM_LIMIT),
+    )(d_out, x_mid, z.reshape(batch, blocks, rows, units), w1, w2, q_t, k_t, v_t, x_in, wqkv_t, wo,
+      *[v.reshape(1, width) for v in (gain2, bias2, gain1, bias1)])
 
 
 def place_results(big, small):
@@ -767,10 +749,9 @@
         q_t, k_t, v_t = feature_rows(q_saved), feature_rows(k_saved), feature_rows(v_saved)
         wqkv_t = jnp.transpose(w_qkv, (0, 2, 3, 1)).reshape(w_qkv.shape[0] * heads * dim, width)
         wo = w_proj.reshape(heads * dim, width)
-        dx1, grad_wfc1, grad_wfc2, ctx_t, ctx, lse, db1, vec = mlp_backward(
-            n_tp, scale * LOG2E, d_out, x_mid, z_saved, w_fc1, w_fc2, q_t, k_t, v_t, ln2_gain, ln2_bias)
-        grad_x, dwqkv, dwo, dbqkv, grad_vecs = attn_backward(
-            n_tp, scale, dx1, x_in, q_t, k_t, v_t, ctx_t, ctx, lse, wqkv_t, wo, ln1_gain, ln1_bias, vec)
+        grad_x, grad_wfc1, grad_wfc2, dwqkv, dwo, db1, dbqkv, grad_vecs = backward(
+            n_tp, scale, d_out, x_mid, z_saved, w_fc1, w_fc2, q_t, k_t, v_t, x_in, wqkv_t, wo,
+            ln2_gain, ln2_bias, ln1_gain, ln1_bias)
         grad_x, grad_wfc1, grad_wfc2, dwqkv, dwo, db1, dbqkv, grad_vecs = place_results(
             (grad_x.reshape(batch * x_in.shape[1], width), grad_wfc1, grad_wfc2, dwqkv, dwo), (db1, dbqkv, grad_vecs))
         grad_x = grad_x.reshape(x_in.shape)

time: 237 us -> 230 us (0.970)
  Pallas kernels: 235 us -> 227 us
    pallas_call x2 -> x1, Pallas kernels: 228 us -> 220 us  [backward(): pl.pallas_call(functools.partial(backward_kernel, n_tp, scale), name='lay...]
where the time goes in v3:
time: 230 us; the launch traced here: 229 us
  Pallas kernels  227 us (99%)
    pallas_call x1, Pallas kernels, backward(): pl.pallas_call(functools.partial(backward_kernel, n_tp, scale), name='lay...  220 us
    pallas_call x1, Pallas kernels, place_results(): pl.pallas_call(kernel, name='place_results', out_shape=[jax.ShapeDtypeStr...  7.26 us

profile of v3, /device:TPU:81, one launch (start us, length us, event | category | flops | bytes accessed | tf_op | source)
XLA Modules:
  0.0 229.4 jit_solution(16125079092321626)
XLA Ops:
  0.6 220.1 %layer_backward.1 = (bf16[2,256,1024]{2,1,0:T(8,128)(2,1)}, f32[1024,512]{1,0:T(8,128)}, f32[512,1024]{1,0:T(8,128)}, f32[384,1024]{1,0:T(8,128)}, f32[128,1024]...) custom-call(bf16[2,256,1024]{2,1,0:T(8,128)(2,1)} %dy_hbm.1, bf16[2,256,1024]{2,1,0:T(8,128)(2,1)} %xm_hbm.1, ...), custom_call_target="tpu_custom_call" | custom-call | tf_op jit(solution)/shard_map/layer_backward/pallas_call | solution.py:672
  220.7 7.3 %place_results.1 = (bf16[512,1024]{1,0:T(8,128)(2,1)}, f32[1024,512]{1,0:T(8,128)}, f32[512,1024]{1,0:T(8,128)}, f32[384,1024]{1,0:T(8,128)}, f32[128,1024]{1,0:...) custom-call(bf16[512,1024]{1,0:T(8,128)(2,1)} %bitcast.26, ...), custom_call_target="tpu_custom_call" | custom-call | tf_op jit(solution)/shard_map/place_results/pallas_call | solution.py:727
  228.0 0.7 reduce
  228.7 0.7 reshape.77

commit v4 on v3

--- a/solution.py
+++ b/solution.py
@@ -14,7 +14,7 @@
 MESH = pl.DeviceIdType.MESH
 F32 = jnp.float32
 BF16 = jnp.bfloat16
-VMEM_LIMIT = 67043328
+VMEM_LIMIT = 227 << 18
 
 NN = (((1,), (0,)), ((), ()))
 NT = (((1,), (1,)), ((), ()))
@@ -327,10 +327,10 @@
 
 def backward_kernel(n_tp, scale, dy_hbm, xm_hbm, z_hbm, w1_hbm, w2_hbm, q_hbm, k_hbm, v_hbm, xi_hbm, wqkv_hbm, wo_hbm,
                     gain2_ref, bias2_ref, gain1_ref, bias1_ref,
-                    dx_hbm, dw1_hbm, dw2_hbm, dwqkv_hbm, dwo_hbm, db1_ref, dbqkv_ref, vecs_ref,
+                    xi, dw1, dw2, dwqkv, dwo, db1_ref, dbqkv_ref, vecs_ref,
                     tok, hb, p_out, p_in, sums, fin, transit,
-                    z, w1, w2, dw1, dw2, own, xm, xi, db1, q_t, k_t, v_t, ctx_t, ctx, lse, acc, head_acc,
-                    wqkv, wo, dqkv, dwqkv, dwo, vacc, vsend, vrecv, vring,
+                    z, w1, w2, own, xm, db1, q_t, k_t, v_t, ctx_t, ctx, lse, acc, head_acc,
+                    wqkv, wo, dqkv, vacc, vsend, vrecv,
                     dy_ss, dy_rs, h2_ss, h2_rs, dx_ss, dx_rs, h1_ss, h1_rs, rs2_ss, rs2_rs, rs1_ss, rs1_rs,
                     lsem, v_ss, v_rs, credit):
     place = Place(n_tp)
@@ -417,7 +417,9 @@
 
     def dw1_pair(r, b):
         def body(p):
-            dw1[...] += mm(hb[CORES * r + p, b], z[b, place.block(r, p)], TN)
+            dz = z[b, place.block(r, p)]
+            for ns in columns(width):
+                dw1[ns, :] += mm(hb[CORES * r + p, b, :, ns], dz, TN)
         loop(CORES, body)
 
     def dw1_own(b):
@@ -558,7 +560,9 @@
 
     def dw_pair(r, b):
         def body(p):
-            dwqkv[...] += mm(dqkv[b, :, span(place.block(r, p), rows)], hb[CORES * r + p, b], NN)
+            part = dqkv[b, :, span(place.block(r, p), rows)]
+            for ns in columns(width):
+                dwqkv[:, ns] += mm(part, hb[CORES * r + p, b, :, ns], NN)
         loop(CORES, body)
 
     def dw_own(b):
@@ -593,19 +597,19 @@
     loop(2, own_body)
     loop(2, near_body)
     loop(2, far_body)
-    recall(4, 2 * blocks - 4)
+    tail = 3
+    recall(4, 2 * blocks - 4 - tail)
+    loop(2, last2)
+    recall(2 * blocks - tail, tail)
     clear(acc)
-    loop(2, last2)
     h2g.relay(0)
     loop(2, dw1_own)
     h2g.relay(1)
     loop(2, dw1_near)
     loop(2, back2)
-    stores = start_copies(((dw2, dw2_hbm),), lsem)
     sc2.finish()
     loop(len(BATCH) * CORES, attend_own)
     loop(2, dw1_far)
-    stores += start_copies(((dw1, dw1_hbm),), lsem.at[pl.ds(1, 1)])
     db1_ref[...] = jnp.sum(db1[...], axis=0, keepdims=True)
     mg.relay(0)
 
@@ -626,23 +630,25 @@
     h1g.relay(1)
     loop(2, dw_near)
     loop(2, back1)
-    stores += start_copies(((xi, dx_hbm), (dwo, dwo_hbm)), lsem.at[pl.ds(2, 2)])
     for k in range(vacc.shape[0]):
         vsend[k:k + 1] = jnp.sum(vacc[k], axis=0, keepdims=True)
     swap = remote(vsend, vrecv, v_ss.at[0], v_rs.at[n_tp], place.partner)
     swap.start()
     swap.wait_recv()
-    vring[place.x] = vsend[...] + vrecv[...]
-    ring = [remote(vring.at[place.x], vring.at[place.x], v_ss.at[r], v_rs.at[place.x], peer)
+
+    def vring(chip):
+        return acc.at[0, span(chip, SUB), pl.ds(0, width)]
+
+    vring(place.x)[...] = vsend[...] + vrecv[...]
+    ring = [remote(vring(place.x), vring(place.x), v_ss.at[r], v_rs.at[place.x], peer)
             for r, peer in zip(RING, (place.right, place.far, place.left))]
     for copy in ring:
         copy.start()
     loop(2, dw_far)
-    stores += start_copies(((dwqkv, dwqkv_hbm),), lsem.at[pl.ds(4, 1)])
     for r in RING:
         other = lax.rem(place.x + r, place.chips)
-        remote(vring.at[other], vring.at[other], v_ss.at[r], v_rs.at[other], place.right).wait_recv()
-    vecs_ref[...] = functools.reduce(jnp.add, [vring[k] for k in range(vring.shape[0])])[:vecs_ref.shape[0]]
+        remote(vring(other), vring(other), v_ss.at[r], v_rs.at[other], place.right).wait_recv()
+    vecs_ref[...] = functools.reduce(jnp.add, [vring(k)[...] for k in range(place.chips)])[:vecs_ref.shape[0]]
     swap.wait_send()
     for copy in ring:
         copy.wait_send()
@@ -651,8 +657,6 @@
         mg.drain(b)
         h1g.drain(b)
     sc1.finish()
-    for store in stores:
-        store.wait()
 
 
 def backward(n_tp, scale, d_out, x_mid, z, w1, w2, q_t, k_t, v_t, x_in, wqkv_t, wo, gain2, bias2, gain1, bias1):
@@ -666,28 +670,24 @@
     slots = pltpu.VMEM((SLOT_END, batch, rows, width), BF16)
     row = pltpu.VMEM((SUB, width), F32)
 
-    def shape(*dims):
-        return jax.ShapeDtypeStruct(dims, F32)
-
     return pl.pallas_call(
         functools.partial(backward_kernel, n_tp, scale),
         name='layer_backward',
-        out_shape=(jax.ShapeDtypeStruct((batch, rows, width), BF16), shape(width, units), shape(units, width),
-                   shape(qkv_rows, width), shape(LANES, width), shape(1, units), shape(1, qkv_rows), shape(6, width)),
+        out_shape=(pltpu.VMEM((batch, rows, width), BF16), pltpu.VMEM((width, units), F32), pltpu.VMEM((units, width), F32),
+                   pltpu.VMEM((qkv_rows, width), F32), pltpu.VMEM((LANES, width), F32),
+                   pltpu.VMEM((1, units), F32), pltpu.VMEM((1, qkv_rows), F32), pltpu.VMEM((6, width), F32)),
         in_specs=[any_spec] * 11 + [vm] * 4,
-        out_specs=(*[any_spec] * 5, vm, vm, vm),
+        out_specs=(vm,) * 8,
         scratch_shapes=[
             slots, slots, *scatter_scratch(rows, width),
             pltpu.VMEM((batch, blocks, rows, units), BF16),
             pltpu.VMEM((width, units), BF16), pltpu.VMEM((units, width), BF16),
-            pltpu.VMEM((width, units), F32), pltpu.VMEM((units, width), F32),
-            pltpu.VMEM((batch, rows, width), F32), *[pltpu.VMEM((batch, rows, width), BF16)] * 2,
+            pltpu.VMEM((batch, rows, width), F32), pltpu.VMEM((batch, rows, width), BF16),
             pltpu.VMEM((SUB, units), F32), *[pltpu.VMEM((batch, LANES, seq), BF16)] * 4,
             pltpu.VMEM((batch, blocks, rows, LANES), F32), pltpu.VMEM((batch, blocks, SUB, rows), F32),
             pltpu.VMEM((len(HEADS), rows, seq), F32), pltpu.VMEM((len(HEADS), rows, LANES), F32),
             pltpu.VMEM((qkv_rows, width), BF16), pltpu.VMEM((LANES, width), BF16), pltpu.VMEM((batch, qkv_rows, seq), BF16),
-            pltpu.VMEM((qkv_rows, width), F32), pltpu.VMEM((LANES, width), F32),
-            pltpu.VMEM((6, SUB, width), F32), row, row, pltpu.VMEM((n_tp // CORES, SUB, width), F32),
+            pltpu.VMEM((6, SUB, width), F32), row, row,
             *copy_sems(*[SLOT_END, SLOT_END + 1] * 4, *[10] * 4),
             pltpu.SemaphoreType.DMA((11,)), pltpu.SemaphoreType.DMA((4,)), pltpu.SemaphoreType.DMA((n_tp + 1,)),
             pltpu.SemaphoreType.REGULAR((batch,)),
@@ -697,42 +697,35 @@
       *[v.reshape(1, width) for v in (gain2, bias2, gain1, bias1)])
 
 
-def place_results(big, small):
-    pieces = 4
+def place_results(big, db1, dbqkv, vecs, bias_shape):
+    count = len(big)
 
     def kernel(*refs):
-        count, rest = len(big), len(small)
-        src, small_in = refs[:count], refs[count:count + rest]
-        dst, small_out = refs[count + rest:2 * count + rest], refs[2 * count + rest:2 * (count + rest)]
-        bufs, sem_in, sem_out = refs[2 * (count + rest):-2], refs[-2], refs[-1]
-        moves = []
-        for i, buf in enumerate(bufs):
-            step = buf.shape[0] // pieces
-            for j in range(pieces):
-                rs = pl.ds(j * step, step)
-                moves.append((pltpu.make_async_copy(src[i].at[rs], buf.at[rs], sem_in.at[i, j]),
-                              pltpu.make_async_copy(buf.at[rs], dst[i].at[rs], sem_out.at[i, j])))
-        for fetch, _ in moves:
-            fetch.start()
-        for ref_in, ref_out in zip(small_in, small_out):
-            ref_out[...] = ref_in[...]
-        for fetch, put in moves:
-            fetch.wait()
-            put.start()
-        for _, put in moves:
-            put.wait()
+        src, (db1_in, dbqkv_in, vecs_in) = refs[:count], refs[count:count + 3]
+        dst, (db1_out, dbqkv_out, vecs_out), sems = refs[count + 3:-4], refs[-4:-1], refs[-1]
+        moves = start_copies(zip(src, dst), sems)
+        db1_out[...] = db1_in[...]
+        vecs_out[...] = vecs_in[...]
+        kinds, heads, dim = bias_shape
+        for i in range(kinds):
+            for h in range(heads):
+                start = (i * heads + h) * dim
+                dbqkv_out[i, h:h + 1] = dbqkv_in[:, start:start + dim]
+        for move in moves:
+            move.wait()
 
     any_spec = pl.BlockSpec(memory_space=pl.ANY)
     vm = pl.BlockSpec(memory_space=pltpu.VMEM)
     return pl.pallas_call(
         kernel,
         name='place_results',
-        out_shape=[jax.ShapeDtypeStruct(v.shape, v.dtype) for v in (*big, *small)],
-        in_specs=[any_spec] * len(big) + [vm] * len(small),
-        out_specs=[any_spec] * len(big) + [vm] * len(small),
-        scratch_shapes=[pltpu.VMEM(v.shape, v.dtype) for v in big] + [pltpu.SemaphoreType.DMA((len(big), pieces))] * 2,
-        compiler_params=pltpu.CompilerParams(vmem_limit_bytes=VMEM_LIMIT),
-    )(*big, *small)
+        out_shape=[jax.ShapeDtypeStruct(v.shape, v.dtype) for v in (*big, db1)]
+        + [jax.ShapeDtypeStruct(bias_shape, F32), jax.ShapeDtypeStruct(vecs.shape, F32)],
+        in_specs=[vm] * (count + 3),
+        out_specs=[any_spec] * count + [vm] * 3,
+        scratch_shapes=[pltpu.SemaphoreType.DMA((count,))],
+        compiler_params=pltpu.CompilerParams(vmem_limit_bytes=8 << 20),
+    )(*[pltpu.with_memory_space_constraint(v, pltpu.VMEM) for v in (*big, db1, dbqkv, vecs)])
 
 
 def solution(mesh):
@@ -752,11 +745,9 @@
         grad_x, grad_wfc1, grad_wfc2, dwqkv, dwo, db1, dbqkv, grad_vecs = backward(
             n_tp, scale, d_out, x_mid, z_saved, w_fc1, w_fc2, q_t, k_t, v_t, x_in, wqkv_t, wo,
             ln2_gain, ln2_bias, ln1_gain, ln1_bias)
-        grad_x, grad_wfc1, grad_wfc2, dwqkv, dwo, db1, dbqkv, grad_vecs = place_results(
-            (grad_x.reshape(batch * x_in.shape[1], width), grad_wfc1, grad_wfc2, dwqkv, dwo), (db1, dbqkv, grad_vecs))
-        grad_x = grad_x.reshape(x_in.shape)
+        grad_x, grad_wfc1, grad_wfc2, dwqkv, dwo, db1, grad_bqkv, grad_vecs = place_results(
+            (grad_x, grad_wfc1, grad_wfc2, dwqkv, dwo), db1, dbqkv, grad_vecs, (w_qkv.shape[0], heads, dim))
         grad_wqkv = jnp.transpose(dwqkv.reshape(-1, heads, dim, width), (0, 3, 1, 2))
-        grad_bqkv = dbqkv.reshape(-1, heads, dim)
         grad_wproj = dwo.reshape(heads, dim, width)
         return grad_x, grad_wqkv, grad_bqkv, grad_wproj, grad_wfc1, db1.reshape(-1), grad_wfc2, grad_vecs
 

time: 230 us -> 218 us (0.948)
  Pallas kernels: 227 us -> 217 us
    pallas_call x1, Pallas kernels: 220 us -> 214 us  [backward(): pl.pallas_call(functools.partial(backward_kernel, n_tp, scale), name='lay...]
    pallas_call x1, Pallas kernels: 7.26 us -> 3.66 us  [place_results(): pl.pallas_call(kernel, name='place_results', out_shape=[jax.ShapeDtypeStr...]
where the time goes in v4:
time: 218 us
  Pallas kernels  217 us (100%)
    pallas_call x1, Pallas kernels, backward(): pl.pallas_call(functools.partial(backward_kernel, n_tp, scale), name='lay...  214 us

profile of v4, /device:TPU:81, one launch (start us, length us, event | category | flops | bytes accessed | tf_op | source)
XLA Modules:
  0.0 218.1 jit_solution(16342325870459668425)
XLA Ops:
  0.6 213.6 %layer_backward.1 = (bf16[2,256,1024]{2,1,0:T(8,128)(2,1)S(1)}, f32[1024,512]{1,0:T(8,128)S(1)}, f32[512,1024]{1,0:T(8,128)S(1)}, f32[384,1024]{1,0:T(8,128)S(1)...) custom-call(bf16[2,256,1024]{2,1,0:T(8,128)(2,1)} %dy_hbm.1, ...), custom_call_target="tpu_custom_call" | custom-call | tf_op jit(solution)/shard_map/layer_backward/pallas_call | solution.py:673
  214.3 3.7 %place_results.1 = (bf16[2,256,1024]{2,1,0:T(8,128)(2,1)}, f32[1024,512]{1,0:T(8,128)}, f32[512,1024]{1,0:T(8,128)}, f32[384,1024]{1,0:T(8,128)}, f32[128,1024]{...) custom-call(bf16[2,256,1024]{2,1,0:T(8,128)(2,1)S(1)} %get-tuple-element.24.refs_0_, ...), custom_call_target="tpu_custom_call" | custom-call | tf_op jit(solution)/shard_map/place_results/pallas_call | solution.py:719

commit v5 on v4

--- a/solution.py
+++ b/solution.py
@@ -514,7 +514,8 @@
             @pl.when((i == 2 * CORES - 1) & (b == 0))
             def _():
                 mg.relay(1)
-                start_h1(0)
+                for k in BATCH:
+                    start_h1(k)
             attend(R_RIGHT + 2 * (i // CORES), lax.rem(i, CORES), b)
         loop(2 * CORES, body)
 
@@ -533,10 +534,6 @@
             mg.relay_far(0)
         mg.wait_shared(R_FAR, b)
         loop(CORES, lambda p: attend(R_FAR, p, b))
-
-        @pl.when(b == 1)
-        def _():
-            sc1.send_last(0)
         mine = span(b, LANES)
         dqkv[b, LANES:2 * LANES] = (acc[0, mine] * scale).astype(BF16)
         dqkv[b, 2 * LANES:] = acc[1, mine].astype(BF16)
@@ -617,15 +614,19 @@
         @pl.when(b == 1)
         def _():
             mg.relay_far(1)
-            start_h1(1)
         attend_near(b)
         attend_far(b)
 
     loop(2, batch)
+    sc1.send_last(0)
     h1g.relay(0)
     loop(2, dw_own)
     ones = jnp.ones((SUB, dqkv.shape[2]), BF16)
-    dbqkv_ref[...] = (mm(ones, dqkv[0], NT) + mm(ones, dqkv[1], NT))[:1]
+    dbqkv = (mm(ones, dqkv[0], NT) + mm(ones, dqkv[1], NT))[:1]
+    for i in range(dbqkv_ref.shape[0]):
+        for h in HEADS:
+            start = i * LANES + h * dim
+            dbqkv_ref[i, h:h + 1] = dbqkv[:, start:start + dim]
     sc1.send_last(1)
     h1g.relay(1)
     loop(2, dw_near)
@@ -675,7 +676,7 @@
         name='layer_backward',
         out_shape=(pltpu.VMEM((batch, rows, width), BF16), pltpu.VMEM((width, units), F32), pltpu.VMEM((units, width), F32),
                    pltpu.VMEM((qkv_rows, width), F32), pltpu.VMEM((LANES, width), F32),
-                   pltpu.VMEM((1, units), F32), pltpu.VMEM((1, qkv_rows), F32), pltpu.VMEM((6, width), F32)),
+                   pltpu.VMEM((1, units), F32), pltpu.VMEM((qkv_rows // LANES, len(HEADS), LANES // len(HEADS)), F32), pltpu.VMEM((6, width), F32)),
         in_specs=[any_spec] * 11 + [vm] * 4,
         out_specs=(vm,) * 8,
         scratch_shapes=[
@@ -697,35 +698,22 @@
       *[v.reshape(1, width) for v in (gain2, bias2, gain1, bias1)])
 
 
-def place_results(big, db1, dbqkv, vecs, bias_shape):
-    count = len(big)
+def place_results(results):
+    count = len(results)
 
     def kernel(*refs):
-        src, (db1_in, dbqkv_in, vecs_in) = refs[:count], refs[count:count + 3]
-        dst, (db1_out, dbqkv_out, vecs_out), sems = refs[count + 3:-4], refs[-4:-1], refs[-1]
-        moves = start_copies(zip(src, dst), sems)
-        db1_out[...] = db1_in[...]
-        vecs_out[...] = vecs_in[...]
-        kinds, heads, dim = bias_shape
-        for i in range(kinds):
-            for h in range(heads):
-                start = (i * heads + h) * dim
-                dbqkv_out[i, h:h + 1] = dbqkv_in[:, start:start + dim]
-        for move in moves:
+        for move in start_copies(zip(refs[:count], refs[count:-1]), refs[-1]):
             move.wait()
 
-    any_spec = pl.BlockSpec(memory_space=pl.ANY)
-    vm = pl.BlockSpec(memory_space=pltpu.VMEM)
     return pl.pallas_call(
         kernel,
         name='place_results',
-        out_shape=[jax.ShapeDtypeStruct(v.shape, v.dtype) for v in (*big, db1)]
-        + [jax.ShapeDtypeStruct(bias_shape, F32), jax.ShapeDtypeStruct(vecs.shape, F32)],
-        in_specs=[vm] * (count + 3),
-        out_specs=[any_spec] * count + [vm] * 3,
+        out_shape=[jax.ShapeDtypeStruct(v.shape, v.dtype) for v in results],
+        in_specs=[pl.BlockSpec(memory_space=pltpu.VMEM)] * count,
+        out_specs=[pl.BlockSpec(memory_space=pl.ANY)] * count,
         scratch_shapes=[pltpu.SemaphoreType.DMA((count,))],
         compiler_params=pltpu.CompilerParams(vmem_limit_bytes=8 << 20),
-    )(*[pltpu.with_memory_space_constraint(v, pltpu.VMEM) for v in (*big, db1, dbqkv, vecs)])
+    )(*[pltpu.with_memory_space_constraint(v, pltpu.VMEM) for v in results])
 
 
 def solution(mesh):
@@ -742,11 +730,9 @@
         q_t, k_t, v_t = feature_rows(q_saved), feature_rows(k_saved), feature_rows(v_saved)
         wqkv_t = jnp.transpose(w_qkv, (0, 2, 3, 1)).reshape(w_qkv.shape[0] * heads * dim, width)
         wo = w_proj.reshape(heads * dim, width)
-        grad_x, grad_wfc1, grad_wfc2, dwqkv, dwo, db1, dbqkv, grad_vecs = backward(
+        grad_x, grad_wfc1, grad_wfc2, dwqkv, dwo, db1, grad_bqkv, grad_vecs = place_results(backward(
             n_tp, scale, d_out, x_mid, z_saved, w_fc1, w_fc2, q_t, k_t, v_t, x_in, wqkv_t, wo,
-            ln2_gain, ln2_bias, ln1_gain, ln1_bias)
-        grad_x, grad_wfc1, grad_wfc2, dwqkv, dwo, db1, grad_bqkv, grad_vecs = place_results(
-            (grad_x, grad_wfc1, grad_wfc2, dwqkv, dwo), db1, dbqkv, grad_vecs, (w_qkv.shape[0], heads, dim))
+            ln2_gain, ln2_bias, ln1_gain, ln1_bias))
         grad_wqkv = jnp.transpose(dwqkv.reshape(-1, heads, dim, width), (0, 3, 1, 2))
         grad_wproj = dwo.reshape(heads, dim, width)
         return grad_x, grad_wqkv, grad_bqkv, grad_wproj, grad_wfc1, db1.reshape(-1), grad_wfc2, grad_vecs

time: 218 us -> 218 us (level)
  no operation moved by 1% of the time
where the time goes in v5:
time: 218 us
  Pallas kernels  217 us (100%)
    pallas_call x1, Pallas kernels, backward(): pl.pallas_call(functools.partial(backward_kernel, n_tp, scale), name='lay...  214 us

profile of v5, /device:TPU:81, one launch (start us, length us, event | category | flops | bytes accessed | tf_op | source)
XLA Modules:
  0.0 217.5 jit_solution(14233622136109900433)
XLA Ops:
  0.6 213.6 %layer_backward.1 = (bf16[2,256,1024]{2,1,0:T(8,128)(2,1)S(1)}, f32[1024,512]{1,0:T(8,128)S(1)}, f32[512,1024]{1,0:T(8,128)S(1)}, f32[384,1024]{1,0:T(8,128)S(1)...) custom-call(bf16[2,256,1024]{2,1,0:T(8,128)(2,1)} %dy_hbm.1, ...), custom_call_target="tpu_custom_call" | custom-call | tf_op jit(solution)/shard_map/layer_backward/pallas_call | solution.py:674
  214.3 3.1 %place_results.1 = (bf16[2,256,1024]{2,1,0:T(8,128)(2,1)}, f32[1024,512]{1,0:T(8,128)}, f32[512,1024]{1,0:T(8,128)}, f32[384,1024]{1,0:T(8,128)}, f32[128,1024]{...) custom-call(bf16[2,256,1024]{2,1,0:T(8,128)(2,1)S(1)} %get-tuple-element.24.refs_0_, ...), custom_call_target="tpu_custom_call" | custom-call | tf_op jit(solution)/shard_map/place_results/pallas_call | solution.py:708
